TPU v7x, 8 devices: a whole 2x2x1 slice. The times are simulated.
8 devices in a mesh: dp: 1 (over z), tp: 8 (over x, y, core).
Axes of the slice: x: 2, y: 2, z: 1, core: 2. Of those that a mesh axis runs over, the one named last changes fastest.
Arguments:
- x: bfloat16 [2560, 3584], P(('dp', 'tp'))
- dy: bfloat16 [2560, 3584], P(('dp', 'tp'))
- gate: bfloat16 [2560, 14336], P('dp', 'tp')
- up: bfloat16 [2560, 14336], P('dp', 'tp')
- w_gate: bfloat16 [3584, 14336], P(None, 'tp')
- w_up: bfloat16 [3584, 14336], P(None, 'tp')
- w_down: bfloat16 [14336, 3584], P('tp')
Outputs:
- output 1: bfloat16 [2560, 3584], P(('dp', 'tp'))
- output 2: bfloat16 [3584, 14336], P('dp', 'tp')
- output 3: bfloat16 [3584, 14336], P('dp', 'tp')
- output 4: bfloat16 [14336, 3584], P(('dp', 'tp'))
All inputs are finite; a program needn't handle non-finite values.
Results may differ from a plain program's by a relative error of at most 0.012.
Values are sent between devices in bfloat16 or wider.
A program may use at most 2 GiB of HBM per device.

v0:
```python
import jax
import jax.numpy as jnp


def act(gate, up):
    return jax.nn.gelu(gate) * up


def solution(mesh):
    def step(x, dy, gate, up, w_gate, w_up, w_down):
        hidden, back = jax.vjp(act, gate.astype(jnp.float32), up.astype(jnp.float32))
        d_hidden = jnp.dot(dy, w_down.T, preferred_element_type=jnp.float32)
        d_gate, d_up = (g.astype(jnp.bfloat16) for g in back(d_hidden))
        dx = jnp.dot(d_gate, w_gate.T) + jnp.dot(d_up, w_up.T)
        groups = mesh.shape["dp"]

        def by_group(a, b):
            a, b = (t.reshape(groups, -1, t.shape[-1]) for t in (a, b))
            product = jnp.einsum("gta,gtb->gab", a, b, preferred_element_type=jnp.float32)
            return product.astype(jnp.bfloat16).reshape(-1, b.shape[-1])

        return dx, by_group(x, d_gate), by_group(x, d_up), by_group(hidden.astype(jnp.bfloat16), dy)

    return step
```

profile of v0, /device:TPU:0, one launch (start us, length us, event | category | flops | bytes accessed | tf_op | source)
XLA Modules:
  0.0 415.3 jit_solution(10663020482951734389)
XLA Ops:
  7.2 0.0 all-gather.7.cloned.1.call-start
  7.2 0.7 all-gather.7.cloned.1.call-update
  7.9 0.0 all-gather.9.cloned.1.call-start
  7.9 0.7 all-gather.9.cloned.1.call-update
  8.6 0.0 reduce-scatter.4.cloned.1.call-start
  8.7 94.7 %all-gather.7.cloned.1.call-done = bf16[2560,3584]{1,0:T(8,128)(2,1)} async-done(((bf16[320,3584]{1,0:T(8,128)(2,1)}), bf16[2560,3584]{1,0:T(8,128)(2,1)}) %all-gather.7.cloned.1.call-update) | async-done | bytes 18350096 | tf_op args[1]
  103.4 52.4 %fusion.4 = (bf16[2560,1792]{1,0:T(8,128)(2,1)}, f32[2560,1792]{1,0:T(8,128)}) fusion(bf16[2560,1792]{1,0:T(8,128)(2,1)} %param.3, bf16[2560,1792]{1,0:T(8,128)(2,1)} %param.2, bf16[2560,3584]{1,0:T(8,128)(2,1)} %all-gather.7.cloned.1.call-done, bf16[1792,3584]{1,0:T(8,128)(2,1)} %param.1), kind=kOutput, calls=%fused_computation.12 | convolution fusion | flops 32988856320 | bytes 77070336 | tf_op jit(solution)/dot_general | solution.py:12
  155.8 40.6 %fusion.21 = bf16[2560,3584]{1,0:T(8,128)(2,1)} fusion(bf16[2560,1792]{1,0:T(8,128)(2,1)} %get-tuple-element.4, bf16[3584,1792]{1,0:T(8,128)(2,1)} %param.4), kind=kOutput, calls=%fused_computation.32 | convolution fusion | flops 32883343360 | bytes 40370176 | tf_op jit(solution)/dot_general | solution.py:14
  196.4 45.0 %convolution_add_fusion = bf16[2560,3584]{1,0:T(8,128)(2,1)} fusion(bf16[2560,3584]{1,0:T(8,128)(2,1)} %fusion.21, bf16[3584,1792]{1,0:T(8,128)(2,1)} %param.5, f32[2560,1792]{1,0:T(8,128)} %get-tuple-element.5, bf16[2560,1792]{1,0:T(8,128)(2,1)} %param.3), kind=kOutput, calls=%fused_computation.8 | convolution fusion | flops 32942981120 | bytes 77070336 | tf_op jit(solution)/dot_general | solution.py:14
  241.4 0.0 reduce-scatter.4.cloned.1.call-update
  241.4 0.0 all-gather.9.cloned.1.call-done
  241.4 40.5 %fusion.10 = bf16[3584,1792]{0,1:T(8,128)(2,1)} fusion(bf16[2560,1792]{1,0:T(8,128)(2,1)} %get-tuple-element.4, bf16[2560,3584]{1,0:T(8,128)(2,1)} %all-gather.9.cloned.1.call-done), kind=kOutput, calls=%fused_computation.22 | convolution fusion | flops 32889765888 | bytes 40370176 | tf_op jit(solution)/gta,gtb->gab/dot_general | solution.py:19
  281.9 18.0 %copy = bf16[3584,1792]{1,0:T(8,128)(2,1)} copy(bf16[3584,1792]{0,1:T(8,128)(2,1)} %fusion.10) | data formatting | bytes 25690112
  299.9 45.6 %fusion.11 = bf16[3584,1792]{0,1:T(8,128)(2,1)} fusion(bf16[2560,3584]{1,0:T(8,128)(2,1)} %all-gather.9.cloned.1.call-done, f32[2560,1792]{1,0:T(8,128)} %get-tuple-element.5, bf16[2560,1792]{1,0:T(8,128)(2,1)} %param.3), kind=kOutput, calls=%fused_computation.23 | convolution fusion | flops 32940228608 | bytes 58720256 | tf_op jit(solution)/gta,gtb->gab/dot_general | solution.py:19
  345.5 18.0 %copy.1 = bf16[3584,1792]{1,0:T(8,128)(2,1)} copy(bf16[3584,1792]{0,1:T(8,128)(2,1)} %fusion.11) | data formatting | bytes 25690112
  363.5 45.3 %convolution_convert_fusion = bf16[1792,3584]{1,0:T(8,128)(2,1)} fusion(bf16[2560,3584]{1,0:T(8,128)(2,1)} %all-gather.7.cloned.1.call-done, bf16[2560,1792]{1,0:T(8,128)(2,1)} %param.2, bf16[2560,1792]{1,0:T(8,128)(2,1)} %param.3), kind=kOutput, calls=%fused_computation.19 | convolution fusion | flops 32944816128 | bytes 49545216 | tf_op jit(solution)/gta,gtb->gab/dot_general | solution.py:19
  408.8 0.0 reduce-scatter.4.cloned.1.call-done
Async XLA Ops:
  7.2 96.2 %all-gather.7.cloned.1.call-start = ((), (), s32[]{:S(2)}) async-start(), calls=%async_computation.1 | async-start | bytes 20643840 | tf_op args[1]
  7.9 233.5 %all-gather.9.cloned.1.call-start = ((), (), s32[]{:S(2)}) async-start(), calls=%async_computation.2 | async-start | bytes 20643840 | tf_op args[0]
  8.6 400.2 %reduce-scatter.4.cloned.1.call-start = ((), (), s32[]{:S(2)}) async-start(), calls=%async_computation.3 | async-start | bytes 20643840
Sparse Core Ops, SparseCore 0:
  9.8 93.5 all-gather.6
  105.2 90.7 all-gather.8
  241.5 114.2 reduce-scatter.3
where the time goes:
time: 416 us; the launch traced here: 415 us
  matrix products  269 us (65%)
  waiting for transfers between devices  96.1 us (23%)
  local copies, waits for them, and re-layouts  36.1 us (9%)
  between operations  13.8 us (3%)
    dot_general x3, matrix products, by_group(): jnp.einsum('gta,gtb->gab', a, b, preferred_element_type=jnp.float32)  131 us
    unnamed x6, waiting for transfers between devices  96.1 us
    dot_general x2, matrix products, step(): dx = jnp.dot(d_gate, w_gate.T) + jnp.dot(d_up, w_up.T)  85.6 us
    dot_general x1, matrix products, step(): d_hidden = jnp.dot(dy, w_down.T, preferred_element_type=jnp.float32)  52.4 us
    unnamed x2, local copies, waits for them, and re-layouts  36.1 us
  transfers between devices with their start and end apart: 3, of which 1 were waited for; matrix products, arithmetic and copies ran while one was open for 74% of the time, Pallas kernels for 0%

commit v1 on v0

v1 whole, which is shorter than its diff:
```python
import functools

import jax
import jax.numpy as jnp
from jax import lax
from jax.experimental import pallas as pl
from jax.experimental.pallas import tpu as pltpu
from jax.sharding import PartitionSpec as P

MESH = pl.DeviceIdType.MESH
ANY = pl.BlockSpec(memory_space=pl.ANY)
VMEM_LIMIT = 60 * 2**20
C0 = 0.7978845608028654
C1 = C0 * 0.044715


def act_and_back(gate, up, d_hidden):
    g = gate.astype(jnp.float32)
    u = up.astype(jnp.float32)
    g2 = g * g
    t = jnp.tanh(g * (C0 + C1 * g2))
    cdf = 0.5 + 0.5 * t
    gelu = g * cdf
    slope = cdf + (0.5 * g) * (1.0 - t * t) * (C0 + (3.0 * C1) * g2)
    return gelu * u, d_hidden * u * slope, d_hidden * gelu


def nt(a, b):
    return lax.dot_general(a, b, (((1,), (1,)), ((), ())), preferred_element_type=jnp.float32)


def tn(a, b):
    return lax.dot_general(a, b, (((0,), (0,)), ((), ())), preferred_element_type=jnp.float32)


def act_body(dy_ref, wd_ref, gate_ref, up_ref, dg_ref, du_ref, h_ref):
    d_hidden = nt(dy_ref[...], wd_ref[...])
    h, dg, du = act_and_back(gate_ref[...], up_ref[...], d_hidden)
    dg_ref[...] = dg.astype(jnp.bfloat16)
    du_ref[...] = du.astype(jnp.bfloat16)
    h_ref[...] = h.astype(jnp.bfloat16)


def dx_body(dg_ref, du_ref, wg_ref, wu_ref, o_ref):
    o_ref[...] = (nt(dg_ref[...], wg_ref[...]) + nt(du_ref[...], wu_ref[...])).astype(jnp.bfloat16)


def front_kernel(
    dy_ref, x_ref, gate_ref, up_ref, wd_ref, wg_ref, wu_ref,
    dyf_ref, xf_ref, dg_ref, du_ref, h_ref, dxp_ref,
    bounce, send_sem, recv_sem, local_sem,
):
    rows, d = dy_ref.shape
    half = rows // 2
    chunk = 2 * rows
    ff = wd_ref.shape[0]
    me = lax.axis_index("tp")
    core = me % 2
    other = me + 1 - 2 * core
    near_y = me + 2 - 4 * ((me // 2) % 2)
    near_x = me + 4 - 8 * (me // 4)
    far = near_y + 4 - 8 * (near_y // 4)

    barrier = pltpu.get_barrier_semaphore()
    for peer in (other, near_y, near_x):
        pl.semaphore_signal(barrier, inc=1, device_id={"tp": peer}, device_id_type=MESH)
    pl.semaphore_wait(barrier, 3)

    def block(owner, part=None):
        if part is None:
            return pl.ds(pl.multiple_of(owner * rows, rows), rows)
        return pl.ds(pl.multiple_of(owner * rows + part * half, half), half)

    class Gather:
        def __init__(self, a, own, full):
            self.a, self.own, self.full = a, own, full
            self.copies = {}

        def send(self, number, src, where, peer):
            copy = pltpu.make_async_remote_copy(
                src_ref=src,
                dst_ref=self.full.at[where, :],
                send_sem=send_sem.at[self.a, number],
                recv_sem=recv_sem.at[self.a, number],
                device_id={"tp": peer},
                device_id_type=MESH,
            )
            copy.start()
            self.copies[number] = copy

        def send_own(self, number, part, peer):
            src = self.own if part is None else self.own.at[pl.ds(part * half, half), :]
            self.send(number, src, block(me, part), peer)

        def pass_on(self, number, owner, part, peer):
            where = block(owner, part)
            self.send(number, self.full.at[where, :], where, peer)

        def arrived(self, *numbers):
            for number in numbers:
                self.copies[number].wait_recv()

        def start(self):
            self.send_own(1, 0, near_x)
            self.send_own(4, 1, near_y)
            self.send_own(2, 1, near_x)
            self.send_own(3, 0, near_y)
            self.send_own(0, None, other)

        def keep_own(self):
            into = pltpu.make_async_copy(self.own, bounce, local_sem.at[self.a, 0])
            into.start()
            into.wait()
            out = pltpu.make_async_copy(bounce, self.full.at[block(me), :], local_sem.at[self.a, 1])
            out.start()
            out.wait()

        def first(self):
            self.arrived(1, 4)
            self.pass_on(5, near_x, 0, near_y)
            self.pass_on(6, near_y, 1, near_x)
            self.pass_on(7, near_x, 0, other)
            self.pass_on(10, near_y, 1, other)

        def second(self):
            self.arrived(2, 3)
            self.pass_on(8, near_x, 1, other)
            self.pass_on(9, near_y, 0, other)

        def third(self):
            self.arrived(5, 6)
            self.pass_on(11, far, 0, other)
            self.pass_on(12, far, 1, other)

        def finish(self):
            for copy in self.copies.values():
                copy.wait_send()

    def rows_of(owner):
        return pl.ds(pl.multiple_of((owner // 2) * chunk, chunk), chunk)

    def act(owner):
        where = rows_of(owner)
        pltpu.emit_pipeline(
            act_body,
            grid=(ff // 256,),
            in_specs=[
                pl.BlockSpec((chunk, d), lambda n: (0, 0)),
                pl.BlockSpec((256, d), lambda n: (n, 0)),
                pl.BlockSpec((chunk, 256), lambda n: (0, n)),
                pl.BlockSpec((chunk, 256), lambda n: (0, n)),
            ],
            out_specs=[pl.BlockSpec((chunk, 256), lambda n: (0, n))] * 3,
        )(
            dyf_ref.at[where, :], wd_ref, gate_ref.at[where, :], up_ref.at[where, :],
            dg_ref.at[where, :], du_ref.at[where, :], h_ref.at[where, :],
        )

    def dx(owner):
        where = rows_of(owner)
        pltpu.emit_pipeline(
            dx_body,
            grid=(d // 512,),
            in_specs=[
                pl.BlockSpec((chunk, ff), lambda n: (0, 0)),
                pl.BlockSpec((chunk, ff), lambda n: (0, 0)),
                pl.BlockSpec((512, ff), lambda n: (n, 0)),
                pl.BlockSpec((512, ff), lambda n: (n, 0)),
            ],
            out_specs=[pl.BlockSpec((chunk, 512), lambda n: (0, n))],
        )(dg_ref.at[where, :], du_ref.at[where, :], wg_ref, wu_ref, dxp_ref.at[where, :])

    dys, xs = Gather(0, dy_ref, dyf_ref), Gather(1, x_ref, xf_ref)
    dys.start()
    dys.keep_own()
    dys.arrived(0)
    act(me)
    dx(me)
    dys.first()
    xs.start()
    dys.second()
    xs.keep_own()
    dys.arrived(7, 8, 9, 10)
    act(near_x)
    act(near_y)
    dys.third()
    dx(near_x)
    dys.arrived(11, 12)
    xs.first()
    act(far)
    dx(near_y)
    xs.second()
    dx(far)
    xs.third()
    xs.arrived(0, 7, 8, 9, 10, 11, 12)
    dys.finish()
    xs.finish()


def front(dy, x, gate, up, wd, wg, wu):
    rows, d = dy.shape
    tokens, ff = gate.shape
    bf16 = jnp.bfloat16
    return pl.pallas_call(
        front_kernel,
        out_shape=[
            jax.ShapeDtypeStruct((tokens, d), bf16),
            jax.ShapeDtypeStruct((tokens, d), bf16),
            jax.ShapeDtypeStruct((tokens, ff), bf16),
            jax.ShapeDtypeStruct((tokens, ff), bf16),
            jax.ShapeDtypeStruct((tokens, ff), bf16),
            jax.ShapeDtypeStruct((tokens, d), bf16),
        ],
        in_specs=[ANY] * 7,
        out_specs=[ANY] * 6,
        scratch_shapes=[
            pltpu.VMEM((rows, d), bf16),
            pltpu.SemaphoreType.DMA((2, 13)),
            pltpu.SemaphoreType.DMA((2, 13)),
            pltpu.SemaphoreType.DMA((2, 2)),
        ],
        compiler_params=pltpu.CompilerParams(
            collective_id=0, has_side_effects=True, vmem_limit_bytes=VMEM_LIMIT
        ),
        cost_estimate=pl.CostEstimate(
            flops=6 * tokens * d * ff, bytes_accessed=300 * 2**20, transcendentals=tokens * ff
        ),
        name="front",
    )(dy, x, gate, up, wd, wg, wu)


def dw_kernel(a_ref, b_ref, o_ref):
    o_ref[...] = tn(a_ref[...], b_ref[...]).astype(o_ref.dtype)


def dw(a, b, tm, tn_):
    tokens, m = a.shape
    n = b.shape[1]
    return pl.pallas_call(
        dw_kernel,
        out_shape=jax.ShapeDtypeStruct((m, n), jnp.bfloat16),
        grid=(m // tm, n // tn_),
        in_specs=[
            pl.BlockSpec((tokens, tm), lambda i, j: (0, i)),
            pl.BlockSpec((tokens, tn_), lambda i, j: (0, j)),
        ],
        out_specs=pl.BlockSpec((tm, tn_), lambda i, j: (i, j)),
        compiler_params=pltpu.CompilerParams(
            dimension_semantics=("arbitrary", "arbitrary"), vmem_limit_bytes=VMEM_LIMIT
        ),
        cost_estimate=pl.CostEstimate(
            flops=2 * tokens * m * n, bytes_accessed=2 * (tokens * m + 2 * tokens * n + m * n), transcendentals=0
        ),
        name="dw",
    )(a, b)


def solution(mesh):
    def step(x, dy, gate, up, wg, wu, wd):
        dyf, xf, dg, du, h, dxp = front(dy, x, gate, up, wd, wg, wu)
        dx = lax.psum_scatter(dxp, "tp", scatter_dimension=0, tiled=True)
        dw_down = dw(h, dyf, 896, 512)
        dw_gate = dw(xf, dg, 512, 896)
        dw_up = dw(xf, du, 512, 896)
        return dx, dw_gate, dw_up, dw_down

    rows, cols, down = P(("dp", "tp"), None), P("dp", "tp"), P("tp", None)
    weight = P(None, "tp")
    return jax.shard_map(
        step,
        mesh=mesh,
        in_specs=(rows, rows, cols, cols, weight, weight, down),
        out_specs=(rows, cols, cols, P(("dp", "tp"), None)),
        check_vma=False,
    )
```

time: 416 us -> 344 us (0.83)
  Pallas kernels: 0 us -> 328 us
  matrix products: 269 us -> 0 us
  waiting for transfers between devices: 96.1 us -> 0.02 us
  local copies, waits for them, and re-layouts: 36.1 us -> 0 us
    pallas_call x0 -> x4, Pallas kernels: none -> 328 us  [the longest x1 191 us: front(): pl.pallas_call(front_kernel, out_shape=[jax.ShapeDtypeStruct((tokens, d),...]
    dot_general x6 -> x0, matrix products: 269 us -> none  [the longest x3 131 us: by_group(): jnp.einsum('gta,gtb->gab', a, b, preferred_element_type=jnp.float32)]
    unnamed x6 -> x1, waiting for transfers between devices: 96.1 us -> 0.02 us
    unnamed x2 -> x0, local copies, waits for them, and re-layouts: 36.1 us -> none
  transfers between devices with their start and end apart: 3 -> 1, of which waited for: 1 -> 0; matrix products, arithmetic and copies ran while one was open for 74% -> 0% of each run, Pallas kernels for 0% -> 40%
where the time goes in v1:
time: 344 us; the launch traced here: 343 us
  Pallas kernels  328 us (95%)
  between operations  14 us (4%)
    pallas_call x1, Pallas kernels, front(): pl.pallas_call(front_kernel, out_shape=[jax.ShapeDtypeStruct((tokens, d),...  191 us
    pallas_call x3, Pallas kernels, dw(): pl.pallas_call(dw_kernel, out_shape=jax.ShapeDtypeStruct((m, n), jnp.bflo...  137 us
  transfers between devices with their start and end apart: 1, of which 0 were waited for; matrix products, arithmetic and copies ran while one was open for 0% of the time, Pallas kernels for 40%

profile of v1, /device:TPU:0, one launch (start us, length us, event | category | flops | bytes accessed | tf_op | source)
XLA Modules:
  0.0 342.6 jit_solution(17146155457011659772)
XLA Ops:
  7.2 0.0 reduce-scatter.2.cloned.1.call-start
  7.2 191.4 %front.1 = (bf16[2560,3584]{1,0:T(8,128)(2,1)}, bf16[2560,3584]{1,0:T(8,128)(2,1)}, bf16[2560,1792]{1,0:T(8,128)(2,1)}, bf16[2560,1792]{1,0:T(8,128)(2,1)}, bf16...) custom-call(bf16[320,3584]{1,0:T(8,128)(2,1)} %dy_ref.1, bf16[320,3584]{1,0:T(8,128)(2,1)} %x_ref.1, ...), custom_call_target="tpu_custom_call" | custom-call | flops 98650030080 | bytes 314572800 | tf_op jit(solution)/shard_map/front/pallas_call | solution.py:204
  198.7 0.0 reduce-scatter.2.cloned.1.call-update
  198.7 48.1 %dw.3 = bf16[3584,1792]{1,0:T(8,128)(2,1)} custom-call(bf16[2560,3584]{1,0:T(8,128)(2,1)} %get-tuple-element.11.a_ref, bf16[2560,1792]{1,0:T(8,128)(2,1)} %get-tuple-element.12.b_ref), custom_call_target="tpu_custom_call" | custom-call | flops 32883343360 | bytes 49545216 | tf_op jit(solution)/shard_map/dw/pallas_call | solution.py:239
  246.8 47.9 %dw.4 = bf16[3584,1792]{1,0:T(8,128)(2,1)} custom-call(bf16[2560,3584]{1,0:T(8,128)(2,1)} %get-tuple-element.11.a_ref, bf16[2560,1792]{1,0:T(8,128)(2,1)} %get-tuple-element.13.b_ref), custom_call_target="tpu_custom_call" | custom-call | flops 32883343360 | bytes 49545216 | tf_op jit(solution)/shard_map/dw/pallas_call | solution.py:239
  294.7 41.1 %dw.5 = bf16[1792,3584]{1,0:T(8,128)(2,1)} custom-call(bf16[2560,1792]{1,0:T(8,128)(2,1)} %get-tuple-element.14.a_ref, bf16[2560,3584]{1,0:T(8,128)(2,1)} %get-tuple-element.15.b_ref), custom_call_target="tpu_custom_call" | custom-call | flops 32883343360 | bytes 58720256 | tf_op jit(solution)/shard_map/dw/pallas_call | solution.py:239
  335.7 0.0 reduce-scatter.2.cloned.1.call-done
Async XLA Ops:
  7.2 328.6 %reduce-scatter.2.cloned.1.call-start = ((), (), s32[]{:S(2)}) async-start(), calls=%async_computation.1 | async-start | bytes 20643840 | tf_op jit(solution)/shard_map/reduce_scatter | solution.py:261
Sparse Core Ops, SparseCore 0:
  198.8 114.2 reduce-scatter.1

commit v2 on v0

v2 whole, which is shorter than its diff:
```python
import functools

import jax
import jax.numpy as jnp
from jax import lax
from jax.experimental import pallas as pl
from jax.experimental.pallas import tpu as pltpu
from jax.sharding import PartitionSpec as P

MESH = pl.DeviceIdType.MESH
ANY = pl.BlockSpec(memory_space=pl.ANY)
VMEM_LIMIT = 60 * 2**20
C0 = 0.7978845608028654
C1 = C0 * 0.044715


def act_and_back(gate, up, d_hidden):
    g = gate.astype(jnp.float32)
    u = up.astype(jnp.float32)
    g2 = g * g
    t = jnp.tanh(g * (C0 + C1 * g2))
    cdf = 0.5 + 0.5 * t
    gelu = g * cdf
    slope = cdf + (0.5 * g) * (1.0 - t * t) * (C0 + (3.0 * C1) * g2)
    return gelu * u, d_hidden * u * slope, d_hidden * gelu


def nt(a, b):
    return lax.dot_general(a, b, (((1,), (1,)), ((), ())), preferred_element_type=jnp.float32)


def tn(a, b):
    return lax.dot_general(a, b, (((0,), (0,)), ((), ())), preferred_element_type=jnp.float32)

TILE = 256
WTILE = 512


def front_kernel(
    dy_ref, x_ref, gate_ref, up_ref, wd_ref, wg_ref, wu_ref,
    dyf_ref, xf_ref, dg_ref, du_ref, h_ref, dwd_ref, give_ref, got_ref, keep_s_ref, keep_n_ref, send_x_ref, send_y_ref,
    dgc, duc, wbuf, send_sem, recv_sem, pair_send, pair_recv, w_sem, dy_sem, wd_sem, gu_sem, out_sem, own_sem,
):
    rows, d = dy_ref.shape
    half = rows // 2
    ff = wd_ref.shape[0]
    tiles, wtiles = ff // TILE, d // WTILE
    me = lax.axis_index("tp")
    other = me + 1 - 2 * (me % 2)
    near_y = me + 2 - 4 * ((me // 2) % 2)
    near_x = me + 4 - 8 * (me // 4)
    far = near_y + 4 - 8 * (near_y // 4)
    across = other - me

    barrier = pltpu.get_barrier_semaphore()
    for peer in (other, near_y, near_x):
        pl.semaphore_signal(barrier, inc=1, device_id={"tp": peer}, device_id_type=MESH)
    pl.semaphore_wait(barrier, 3)

    def block(owner, part=None):
        if part is None:
            return pl.ds(pl.multiple_of(owner * rows, rows), rows)
        return pl.ds(pl.multiple_of(owner * rows + part * half, half), half)

    routes = [
        (me, None, other),
        (me, 0, near_x), (me, 1, near_x), (me, 0, near_y), (me, 1, near_y),
        (near_x, 0, near_y), (near_y, 1, near_x),
        (near_x, 0, other), (near_x, 1, other), (near_y, 0, other), (near_y, 1, other),
        (far, 0, other), (far, 1, other),
    ]
    places = [block(owner, part) for owner, part, _ in routes]

    class Gather:
        def __init__(self, a, own, full):
            self.a, self.own, self.full = a, own, full

        def copy(self, number):
            _, part, peer = routes[number]
            if number < 5:
                src = self.own if part is None else self.own.at[pl.ds(part * half, half), :]
            else:
                src = self.full.at[places[number], :]
            return pltpu.make_async_remote_copy(
                src_ref=src,
                dst_ref=self.full.at[places[number], :],
                send_sem=send_sem.at[self.a, number],
                recv_sem=recv_sem.at[self.a, number],
                device_id={"tp": peer},
                device_id_type=MESH,
            )

        def send(self, *numbers):
            for number in numbers:
                self.copy(number).start()

        def arrived(self, *numbers):
            for number in numbers:
                self.copy(number).wait_recv()

        def finish(self):
            for number in range(len(routes)):
                self.copy(number).wait_send()

    dys, xs = Gather(0, dy_ref, dyf_ref), Gather(1, x_ref, xf_ref)

    def pair(p):
        return pltpu.make_async_remote_copy(
            src_ref=give_ref.at[p],
            dst_ref=got_ref.at[p],
            send_sem=pair_send.at[p],
            recv_sem=pair_recv.at[p],
            device_id={"tp": other},
            device_id_type=MESH,
        )

    pieces = [
        [(other, 0), (other, 1), (me, 0), (me, 1)],
        [(near_x + across, 0), (near_y + across, 1), (near_x, 0), (near_y, 1)],
        [(near_x + across, 1), (near_y + across, 0), (near_x, 1), (near_y, 0)],
        [(far + across, 0), (far + across, 1), (far, 0), (far, 1)],
    ]
    where = [[block(*piece) for piece in part] for part in pieces]

    def w_copies(tile, slot):
        at = pl.ds(pl.multiple_of(tile * WTILE, WTILE), WTILE)
        return [
            pltpu.make_async_copy(ref.at[at, :], wbuf.at[slot, i], w_sem.at[slot, i]) for i, ref in enumerate((wg_ref, wu_ref))
        ]

    def dx(k, last, parts, ins, outs, store, hook_at=None, hook=None):
        def body(step, *refs):
            n = step.index[0]
            slot = lax.rem(wtiles * k + n, 2)
            for copy in w_copies(n, slot):
                copy.wait()

            def ahead():
                for copy in w_copies(lax.rem(n + 1, wtiles), 1 - slot):
                    copy.start()

            if last:
                pl.when(n < wtiles - 1)(ahead)
            else:
                ahead()
            if hook is not None:
                pl.when(n == hook_at)(hook)
            sums = [
                nt(dgc[p, pl.ds(first, count), :], wbuf[slot, 0]) + nt(duc[p, pl.ds(first, count), :], wbuf[slot, 1])
                for p, first, count in parts
            ]
            store(sums, refs[: len(ins)], refs[len(ins) :])

        spec = pl.BlockSpec((rows, WTILE), lambda n: (0, n))
        pltpu.emit_pipeline(
            body, grid=(wtiles,), in_specs=[spec] * len(ins), out_specs=[spec] * len(outs), _explicit_indices=True
        )(*ins, *outs)

    def give(k, p, hook_at=None, hook=None):
        def store(sums, _, outs):
            outs[0][...] = sums[0].astype(jnp.bfloat16)

        dx(k, False, [(p, 0, rows)], [], [give_ref.at[p]], store, hook_at, hook)
        pair(p).start()

    def with_acts(dyc, wdb, gub, hc, acc):
        def dy_load(p, i):
            if p == 0 and i >= 2:
                src = dy_ref.at[pl.ds((i - 2) * half, half), :]
            else:
                src = dyf_ref.at[where[p][i], :]
            return pltpu.make_async_copy(src, dyc.at[p % 2, pl.ds(i * half, half), :], dy_sem.at[p % 2, i])

        def wd_copy(tile, slot):
            at = pl.ds(pl.multiple_of(tile * TILE, TILE), TILE)
            return pltpu.make_async_copy(wd_ref.at[at, :], wdb.at[slot], wd_sem.at[slot])

        def gu_copies(p, tile, slot):
            at = pl.ds(pl.multiple_of(tile * TILE, TILE), TILE)
            return [
                pltpu.make_async_copy(
                    ref.at[where[p][i], at], gub.at[slot, j, pl.ds(i * half, half), :], gu_sem.at[slot, j, i]
                )
                for j, ref in enumerate((gate_ref, up_ref))
                for i in range(4)
            ]

        def out_copies(p):
            full = ((dgc.at[p], dg_ref), (duc.at[p], du_ref), (hc, h_ref))
            return [
                pltpu.make_async_copy(src.at[pl.ds(i * half, half), :], ref.at[where[p][i], :], out_sem.at[j, i])
                for j, (src, ref) in enumerate(full)
                for i in range(4)
            ]

        def act(p):
            for i in range(4):
                dy_load(p, i).wait()
            if p > 0:
                for copy in out_copies(p - 1):
                    copy.wait()

            def product(slot):
                acc[...] = nt(dyc[p % 2], wdb[slot])

            def elementwise(n, slot):
                at = pl.ds(pl.multiple_of(n * TILE, TILE), TILE)
                h, dg, du = act_and_back(gub[slot, 0], gub[slot, 1], acc[...])
                dgc[p, :, at] = dg.astype(jnp.bfloat16)
                duc[p, :, at] = du.astype(jnp.bfloat16)
                hc[:, at] = h.astype(jnp.bfloat16)

            def fetch(n, ahead_gu):
                count = tiles * p + n
                wd_copy(n, lax.rem(count, 2)).wait()
                for copy in gu_copies(p, n, lax.rem(count, 3)):
                    copy.wait()
                if p < 3:
                    wd_copy(lax.rem(n + 1, tiles), lax.rem(count + 1, 2)).start()
                else:
                    pl.when(n < tiles - 1)(lambda: wd_copy(n + 1, lax.rem(count + 1, 2)).start())
                if ahead_gu:
                    for copy in gu_copies(p, n + 1, lax.rem(count + 1, 3)):
                        copy.start()

            fetch(jnp.int32(0), True)
            product((tiles * p) % 2)

            def later(n, carry):
                count = tiles * p + n
                fetch(n, False)

                @pl.when(n < tiles - 1)
                def _():
                    for copy in gu_copies(p, n + 1, lax.rem(count + 1, 3)):
                        copy.start()

                elementwise(n - 1, lax.rem(count - 1, 3))
                product(lax.rem(count, 2))
                return carry

            lax.fori_loop(1, tiles, later, 0)
            if p < 3:
                for copy in gu_copies(p + 1, 0, (tiles * (p + 1)) % 3):
                    copy.start()
            elementwise(tiles - 1, (tiles * (p + 1) - 1) % 3)
            for copy in out_copies(p):
                copy.start()

        def own_x(leg):
            hold = dyc.at[1, pl.ds(0, rows), :]
            src, dst = ((x_ref, hold), (hold, xf_ref.at[block(me), :]))[leg]
            return pltpu.make_async_copy(src, dst, own_sem.at[leg])

        def own_dy():
            return pltpu.make_async_copy(dyc.at[0, pl.ds(rows, rows), :], dyf_ref.at[block(me), :], own_sem.at[2])

        dys.send(0, 1, 4, 2, 3)
        dy_load(0, 2).start()
        dy_load(0, 3).start()
        wd_copy(0, 0).start()
        for copy in gu_copies(0, 0, 0):
            copy.start()
        own_x(0).start()
        for copy in w_copies(0, 0):
            copy.start()
        dys.arrived(0)
        dy_load(0, 0).start()
        dy_load(0, 1).start()
        act(0)
        own_dy().start()
        own_x(0).wait()
        own_x(1).start()

        def first_halves():
            dys.arrived(1, 4)
            dys.send(5, 6, 7, 10)
            xs.send(0, 1, 4, 2, 3)

        def store_s(sums, _, outs):
            outs[0][...] = sums[0].astype(jnp.bfloat16)
            outs[1][...] = sums[1]

        dx(0, False, [(0, 0, rows), (0, rows, rows)], [], [give_ref.at[0], keep_s_ref], store_s, 4, first_halves)
        pair(0).start()
        own_x(1).wait()
        dys.arrived(7, 10)
        for i in range(4):
            dy_load(1, i).start()
        act(1)
        dys.arrived(2, 3)
        dys.send(8, 9)
        give(1, 1)
        own_dy().wait()
        dys.arrived(8, 9)
        for i in range(4):
            dy_load(2, i).start()
        act(2)

        def far_halves():
            dys.arrived(5, 6)
            dys.send(11, 12)

        give(2, 2, 3, far_halves)
        dys.arrived(11, 12)
        for i in range(4):
            dy_load(3, i).start()
        act(3)
        give(3, 3)
        for copy in out_copies(3):
            copy.wait()

    pl.run_scoped(
        with_acts,
        pltpu.VMEM((2, 2 * rows, d), jnp.bfloat16),
        pltpu.VMEM((2, TILE, d), jnp.bfloat16),
        pltpu.VMEM((3, 2, 2 * rows, TILE), jnp.bfloat16),
        pltpu.VMEM((2 * rows, ff), jnp.bfloat16),
        pltpu.VMEM((2 * rows, TILE), jnp.float32),
    )

    xs.arrived(1, 4)
    xs.send(5, 6, 7, 10)

    def down(h_tile, dy_tile, o_ref):
        o_ref[...] = tn(h_tile[...], dy_tile[...]).astype(jnp.bfloat16)

    tokens = dyf_ref.shape[0]
    pltpu.emit_pipeline(
        down,
        grid=(ff // 896, d // 512),
        in_specs=[
            pl.BlockSpec((tokens, 896), lambda i, j: (0, i)),
            pl.BlockSpec((tokens, 512), lambda i, j: (0, j)),
        ],
        out_specs=[pl.BlockSpec((896, 512), lambda i, j: (i, j))],
    )(h_ref, dyf_ref, dwd_ref)

    xs.arrived(2, 3)
    xs.send(8, 9)
    for p in (1, 2, 3):
        pair(p).wait_recv()

    def store_kept(sums, gots, outs):
        near0, near1, far_sum = (s + g[...].astype(jnp.float32) for s, g in zip(sums, gots))
        to_x, to_y, kept = outs
        to_x[pl.ds(0, half), :] = near0[:half].astype(jnp.bfloat16)
        to_y[pl.ds(0, half), :] = near0[half:].astype(jnp.bfloat16)
        kept[...] = near1
        to_x[pl.ds(half, half), :] = far_sum[:half].astype(jnp.bfloat16)
        to_y[pl.ds(half, half), :] = far_sum[half:].astype(jnp.bfloat16)

    def far_x():
        xs.arrived(5, 6)
        xs.send(11, 12)

    dx(
        4, True, [(p, rows, rows) for p in (1, 2, 3)], [got_ref.at[p] for p in (1, 2, 3)],
        [send_x_ref, send_y_ref, keep_n_ref], store_kept, wtiles - 2, far_x,
    )
    xs.arrived(0, 7, 8, 9, 10, 11, 12)
    pair(0).wait_recv()
    for p in range(4):
        pair(p).wait_send()
    dys.finish()
    xs.finish()


def front(dy, x, gate, up, wd, wg, wu):
    rows, d = dy.shape
    tokens, ff = gate.shape
    bf16, f32 = jnp.bfloat16, jnp.float32
    shapes = [
        ((tokens, d), bf16), ((tokens, d), bf16), ((tokens, ff), bf16), ((tokens, ff), bf16), ((tokens, ff), bf16),
        ((ff, d), bf16), ((4, rows, d), bf16), ((4, rows, d), bf16), ((rows, d), f32), ((rows, d), f32),
        ((rows, d), bf16), ((rows, d), bf16),
    ]
    dma = pltpu.SemaphoreType.DMA
    return pl.pallas_call(
        front_kernel,
        out_shape=[jax.ShapeDtypeStruct(*s) for s in shapes],
        in_specs=[ANY] * 7,
        out_specs=[ANY] * len(shapes),
        scratch_shapes=[
            pltpu.VMEM((4, 2 * rows, ff), bf16),
            pltpu.VMEM((4, 2 * rows, ff), bf16),
            pltpu.VMEM((2, 2, WTILE, ff), bf16),
            dma((2, 13)), dma((2, 13)), dma((4,)), dma((4,)), dma((2, 2)),
            dma((2, 4)), dma((2,)), dma((3, 2, 4)), dma((3, 4)), dma((3,)),
        ],
        compiler_params=pltpu.CompilerParams(
            collective_id=0, has_side_effects=True, vmem_limit_bytes=VMEM_LIMIT
        ),
        cost_estimate=pl.CostEstimate(
            flops=8 * tokens * d * ff, bytes_accessed=300 * 2**20, transcendentals=tokens * ff
        ),
        name="front",
    )(dy, x, gate, up, wd, wg, wu)


def dw_kernel(a_ref, b_hbm, o_ref, b, sems):
    n = b.shape[1]
    cuts = [(j * 256, 256) for j in range(n // 256)]

    def load(j):
        at = pl.ds(cuts[j][0], cuts[j][1])
        return pltpu.make_async_copy(b_hbm.at[:, at], b.at[:, at], sems.at[j])

    @pl.when(pl.program_id(0) == 0)
    def _():
        for j in range(len(cuts)):
            load(j).start()
        for j, (first, count) in enumerate(cuts):
            load(j).wait()
            o_ref[:, first : first + count] = tn(a_ref[...], b[:, first : first + count]).astype(o_ref.dtype)

    @pl.when(pl.program_id(0) > 0)
    def _():
        o_ref[...] = tn(a_ref[...], b[...]).astype(o_ref.dtype)


def dw(a, b, tm=256):
    tokens, m = a.shape
    n = b.shape[1]
    return pl.pallas_call(
        dw_kernel,
        out_shape=jax.ShapeDtypeStruct((m, n), jnp.bfloat16),
        grid=(m // tm,),
        in_specs=[pl.BlockSpec((tokens, tm), lambda i: (0, i)), ANY],
        out_specs=pl.BlockSpec((tm, n), lambda i: (i, 0)),
        scratch_shapes=[pltpu.VMEM((tokens, n), jnp.bfloat16), pltpu.SemaphoreType.DMA((n // 256,))],
        compiler_params=pltpu.CompilerParams(dimension_semantics=("arbitrary",), vmem_limit_bytes=VMEM_LIMIT),
        cost_estimate=pl.CostEstimate(
            flops=2 * tokens * m * n, bytes_accessed=2 * (tokens * m + tokens * n + m * n), transcendentals=0
        ),
        name="dw",
    )(a, b)


def solution(mesh):
    devices = mesh.shape["tp"]
    to_x = [(i, i ^ 4) for i in range(devices)]
    to_y = [(i, i ^ 2) for i in range(devices)]

    def step(x, dy, gate, up, wg, wu, wd):
        bf16, f32 = jnp.bfloat16, jnp.float32
        half = x.shape[0] // 2
        _, xf, dg, du, _, dw_down, _, got, keep_s, keep_n, send_x, send_y = front(dy, x, gate, up, wd, wg, wu)
        from_x = lax.ppermute(send_x, "tp", to_x)
        from_y = lax.ppermute(send_y, "tp", to_y)
        dw_gate = dw(xf, dg)
        on_y = (keep_n[half:] + from_x[half:].astype(f32)).astype(bf16)
        on_x = (keep_n[:half] + from_y[half:].astype(f32)).astype(bf16)
        du, on_y, on_x = lax.optimization_barrier((du, on_y, on_x))
        last_y = lax.ppermute(on_y, "tp", to_y)
        last_x = lax.ppermute(on_x, "tp", to_x)
        dw_up = dw(xf, du)
        kept = keep_s + got[0].astype(f32)
        dx = jnp.concatenate(
            [
                kept[:half] + from_x[:half].astype(f32) + last_y.astype(f32),
                kept[half:] + from_y[:half].astype(f32) + last_x.astype(f32),
            ]
        ).astype(bf16)
        return dx, dw_gate, dw_up, dw_down

    rows, cols, down = P(("dp", "tp"), None), P("dp", "tp"), P("tp", None)
    weight = P(None, "tp")
    return jax.shard_map(
        step,
        mesh=mesh,
        in_specs=(rows, rows, cols, cols, weight, weight, down),
        out_specs=(rows, cols, cols, P(("dp", "tp"), None)),
        check_vma=False,
    )
```

time: 416 us -> 331 us (0.80)
  Pallas kernels: 0 us -> 297 us
  matrix products: 269 us -> 0 us
  waiting for transfers between devices: 96.1 us -> 2.51 us
  local copies, waits for them, and re-layouts: 36.1 us -> 10.6 us
  other arithmetic: 0 us -> 15.6 us
  between operations: 13.8 us -> 0.68 us
  starting transfers between devices: 0.11 us -> 4.38 us
    pallas_call x0 -> x3, Pallas kernels: none -> 297 us  [the longest x1 210 us: front(): pl.pallas_call(front_kernel, out_shape=[jax.ShapeDtypeStruct(*s) for s in...]
    dot_general x6 -> x0, matrix products: 269 us -> none  [the longest x3 131 us: by_group(): jnp.einsum('gta,gtb->gab', a, b, preferred_element_type=jnp.float32)]
    unnamed x6 -> x0, waiting for transfers between devices: 96.1 us -> none
    unnamed x2 -> x1, local copies, waits for them, and re-layouts: 36.1 us -> 10.6 us
    add x0 -> x1, other arithmetic: none -> 5.71 us  [step(): kept = keep_s + got[0].astype(f32)]
    ppermute x0 -> x4, starting transfers between devices: none -> 4.38 us  [the longest x1 1.51 us: step(): from_x = lax.ppermute(send_x, 'tp', to_x)]
    convert_element_type x0 -> x1, other arithmetic: none -> 4.2 us  [step(): on_x = (keep_n[:half] + from_y[half:].astype(f32)).astype(bf16)]
  transfers between devices with their start and end apart: 3 -> 4, of which waited for: 1 -> 2; matrix products, arithmetic and copies ran while one was open for 74% -> 2% of each run, Pallas kernels for 0% -> 26%
where the time goes in v2:
time: 331 us
  Pallas kernels  297 us (90%)
  other arithmetic  15.6 us (5%)
  local copies, waits for them, and re-layouts  10.6 us (3%)
  starting transfers between devices  4.38 us (1%)
    pallas_call x1, Pallas kernels, front(): pl.pallas_call(front_kernel, out_shape=[jax.ShapeDtypeStruct(*s) for s in...  210 us
    pallas_call x2, Pallas kernels, dw(): pl.pallas_call(dw_kernel, out_shape=jax.ShapeDtypeStruct((m, n), jnp.bflo...  86.3 us
    unnamed x1, local copies, waits for them, and re-layouts  10.6 us
  transfers between devices with their start and end apart: 4, of which 2 were waited for; matrix products, arithmetic and copies ran while one was open for 2% of the time, Pallas kernels for 26%

profile of v2, /device:TPU:0, one launch (start us, length us, event | category | flops | bytes accessed | tf_op | source)
XLA Modules:
  0.0 330.6 jit_solution(11674998743901968460)
XLA Ops:
  0.6 210.5 %front.1 = (bf16[2560,3584]{1,0:T(8,128)(2,1)}, bf16[2560,3584]{1,0:T(8,128)(2,1)}, bf16[2560,1792]{1,0:T(8,128)(2,1)}, bf16[2560,1792]{1,0:T(8,128)(2,1)}, bf16...) custom-call(bf16[320,3584]{1,0:T(8,128)(2,1)} %dy_ref.1, ...), custom_call_target="tpu_custom_call" | custom-call | flops 131533373440 | bytes 314572800 | tf_op jit(solution)/shard_map/front/pallas_call | solution.py:379
  211.1 1.5 collective-permute-start
  212.6 0.9 collective-permute-start.1
  213.5 5.7 %convert_add_fusion = f32[320,3584]{1,0:T(8,128)} fusion(f32[320,3584]{1,0:T(8,128)} %get-tuple-element.16, bf16[4,320,3584]{2,1,0:T(8,128)(2,1)} %get-tuple-element.17), kind=kLoop, calls=%fused_computation | loop fusion | flops 2293760 | bytes 11468800 | tf_op jit(solution)/shard_map/add | solution.py:458
  219.2 43.2 %dw.2 = bf16[3584,1792]{1,0:T(8,128)(2,1)} custom-call(bf16[2560,3584]{1,0:T(8,128)(2,1)} %get-tuple-element.24.a_ref, bf16[2560,1792]{1,0:T(8,128)(2,1)} %get-tuple-element.25.b_hbm), custom_call_target="tpu_custom_call" | custom-call | flops 32883343360 | bytes 40370176 | tf_op jit(solution)/shard_map/dw/pallas_call | solution.py:425
  262.4 1.3 collective-permute-done
  263.7 1.2 collective-permute-done.1
  264.9 4.2 %add_convert_fusion = (bf16[160,3584]{1,0:T(8,128)(2,1)S(1)}, bf16[160,3584]{1,0:T(8,128)(2,1)}) fusion(f32[320,3584]{1,0:T(8,128)} %get-tuple-element.20, bf16[320,3584]{1,0:T(8,128)(2,1)} %collective-permute-done.1, bf16[320,3584]{1,0:T(8,128)(2,1)S(1)} %collective-permute-done), kind=kLoop, calls=%fused_computation.8 | loop fusion | flops 3440640 | bytes 9175040 | tf_op jit(solution)/shard_map/convert_element_type | solution.py:453
  269.1 0.5 collective-permute-start.2
  269.6 1.5 collective-permute-start.3
  271.1 43.2 %dw.3 = bf16[3584,1792]{1,0:T(8,128)(2,1)} custom-call(bf16[2560,3584]{1,0:T(8,128)(2,1)} %get-tuple-element.24.a_ref, bf16[2560,1792]{1,0:T(8,128)(2,1)} %get-tuple-element.26.b_hbm), custom_call_target="tpu_custom_call" | custom-call | flops 32883343360 | bytes 40370176 | tf_op jit(solution)/shard_map/dw/pallas_call | solution.py:425
  314.3 0.0 collective-permute-done.2
  314.3 0.0 collective-permute-done.3
  314.3 4.1 %fusion.3 = (bf16[160,3584]{1,0:T(8,128)(2,1)S(1)}, bf16[160,3584]{1,0:T(8,128)(2,1)S(1)}) fusion(f32[320,3584]{1,0:T(8,128)} %convert_add_fusion, bf16[160,3584]{1,0:T(8,128)(2,1)} %collective-permute-done.2, bf16[320,3584]{1,0:T(8,128)(2,1)S(1)} %collective-permute-done, bf16[160,3584]{1,0:T(8,128)(2,1)} %collective-permute-done.3, ...), kind=kLoop, calls=%fused_computation.6 | loop fusion | flops 5734400 | bytes 11468800 | tf_op jit(solution)/shard_map/convert.1
  318.4 1.5 pad_maximum_fusion
  320.0 10.6 %copy.12 = bf16[1792,3584]{1,0:T(8,128)(2,1)} copy(bf16[1792,3584]{1,0:T(8,128)(2,1)} %get-tuple-element.39) | data formatting | bytes 25690112
Async XLA Ops:
  211.1 52.6 %collective-permute-start = (bf16[320,3584]{1,0:T(8,128)(2,1)}, bf16[320,3584]{1,0:T(8,128)(2,1)S(1)}, u32[]{:S(2)}, u32[]{:S(2)}) collective-permute-start(bf16[320,3584]{1,0:T(8,128)(2,1)} %get-tuple-element.18), channel_id=1, source_target_pairs={{0,4},{1,5},{2,6},{3,7},{4,0},{5,1},{6,2},{7,3}} | collective-permute-start | bytes 6881288 | tf_op jit(solution)/shard_map/ppermute | solution.py:449
  212.6 52.3 %collective-permute-start.1 = (bf16[320,3584]{1,0:T(8,128)(2,1)}, bf16[320,3584]{1,0:T(8,128)(2,1)}, u32[]{:S(2)}, u32[]{:S(2)}) collective-permute-start(bf16[320,3584]{1,0:T(8,128)(2,1)} %get-tuple-element.21), channel_id=1, source_target_pairs={{0,2},{1,3},{2,0},{3,1},{4,6},{5,7},{6,4},{7,5}} | collective-permute-start | bytes 6881288 | tf_op jit(solution)/shard_map/ppermute | solution.py:450
  269.1 45.2 %collective-permute-start.2 = (bf16[160,3584]{1,0:T(8,128)(2,1)}, bf16[160,3584]{1,0:T(8,128)(2,1)}, u32[]{:S(2)}, u32[]{:S(2)}) collective-permute-start(bf16[160,3584]{1,0:T(8,128)(2,1)} %get-tuple-element.22), channel_id=1, source_target_pairs={{0,2},{1,3},{2,0},{3,1},{4,6},{5,7},{6,4},{7,5}} | collective-permute-start | bytes 3440648 | tf_op jit(solution)/shard_map/ppermute | solution.py:455
  269.6 44.7 %collective-permute-start.3 = (bf16[160,3584]{1,0:T(8,128)(2,1)S(1)}, bf16[160,3584]{1,0:T(8,128)(2,1)}, u32[]{:S(2)}, u32[]{:S(2)}) collective-permute-start(bf16[160,3584]{1,0:T(8,128)(2,1)S(1)} %get-tuple-element.23), channel_id=1, source_target_pairs={{0,4},{1,5},{2,6},{3,7},{4,0},{5,1},{6,2},{7,3}} | collective-permute-start | bytes 3440648 | tf_op jit(solution)/shard_map/ppermute | solution.py:456

commit v3 on v2

--- a/solution.py
+++ b/solution.py
@@ -1,5 +1,3 @@
-import functools
-
 import jax
 import jax.numpy as jnp
 from jax import lax
@@ -128,7 +126,7 @@
             pltpu.make_async_copy(ref.at[at, :], wbuf.at[slot, i], w_sem.at[slot, i]) for i, ref in enumerate((wg_ref, wu_ref))
         ]
 
-    def dx(k, last, parts, ins, outs, store, hook_at=None, hook=None):
+    def dx(k, last, parts, ins, outs, store, hooks):
         def body(step, *refs):
             n = step.index[0]
             slot = lax.rem(wtiles * k + n, 2)
@@ -143,8 +141,8 @@
                 pl.when(n < wtiles - 1)(ahead)
             else:
                 ahead()
-            if hook is not None:
-                pl.when(n == hook_at)(hook)
+            for at, hook in hooks.items():
+                pl.when(n == at)(hook)
             sums = [
                 nt(dgc[p, pl.ds(first, count), :], wbuf[slot, 0]) + nt(duc[p, pl.ds(first, count), :], wbuf[slot, 1])
                 for p, first, count in parts
@@ -156,31 +154,28 @@
             body, grid=(wtiles,), in_specs=[spec] * len(ins), out_specs=[spec] * len(outs), _explicit_indices=True
         )(*ins, *outs)
 
-    def give(k, p, hook_at=None, hook=None):
+    def give(k, p, hooks={}):
         def store(sums, _, outs):
             outs[0][...] = sums[0].astype(jnp.bfloat16)
 
-        dx(k, False, [(p, 0, rows)], [], [give_ref.at[p]], store, hook_at, hook)
+        dx(k, False, [(p, 0, rows)], [], [give_ref.at[p]], store, hooks)
         pair(p).start()
 
-    def with_acts(dyc, wdb, gub, hc, acc):
+    def with_acts(dyc, wdb, gub, hc):
         def dy_load(p, i):
             if p == 0 and i >= 2:
                 src = dy_ref.at[pl.ds((i - 2) * half, half), :]
             else:
                 src = dyf_ref.at[where[p][i], :]
-            return pltpu.make_async_copy(src, dyc.at[p % 2, pl.ds(i * half, half), :], dy_sem.at[p % 2, i])
-
-        def wd_copy(tile, slot):
-            at = pl.ds(pl.multiple_of(tile * TILE, TILE), TILE)
-            return pltpu.make_async_copy(wd_ref.at[at, :], wdb.at[slot], wd_sem.at[slot])
-
-        def gu_copies(p, tile, slot):
-            at = pl.ds(pl.multiple_of(tile * TILE, TILE), TILE)
+            return pltpu.make_async_copy(src, dyc.at[pl.ds(i * half, half), :], dy_sem.at[i])
+
+        def wd_copy(j):
+            at = pl.ds(pl.multiple_of(j * TILE, TILE), TILE)
+            return pltpu.make_async_copy(wd_ref.at[at, :], wdb.at[at, :], wd_sem.at[j])
+
+        def gu_copies(p):
             return [
-                pltpu.make_async_copy(
-                    ref.at[where[p][i], at], gub.at[slot, j, pl.ds(i * half, half), :], gu_sem.at[slot, j, i]
-                )
+                pltpu.make_async_copy(ref.at[where[p][i], :], gub.at[j, pl.ds(i * half, half), :], gu_sem.at[j, i])
                 for j, ref in enumerate((gate_ref, up_ref))
                 for i in range(4)
             ]
@@ -196,72 +191,54 @@
         def act(p):
             for i in range(4):
                 dy_load(p, i).wait()
+            for copy in gu_copies(p):
+                copy.wait()
             if p > 0:
                 for copy in out_copies(p - 1):
                     copy.wait()
 
-            def product(slot):
-                acc[...] = nt(dyc[p % 2], wdb[slot])
-
-            def elementwise(n, slot):
-                at = pl.ds(pl.multiple_of(n * TILE, TILE), TILE)
-                h, dg, du = act_and_back(gub[slot, 0], gub[slot, 1], acc[...])
+            def tile(j, carry):
+                if p == 0:
+                    wd_copy(j).wait()
+                at = pl.ds(pl.multiple_of(j * TILE, TILE), TILE)
+                d_hidden = nt(dyc[...], wdb[at, :])
+                h, dg, du = act_and_back(gub[0, :, at], gub[1, :, at], d_hidden)
                 dgc[p, :, at] = dg.astype(jnp.bfloat16)
                 duc[p, :, at] = du.astype(jnp.bfloat16)
                 hc[:, at] = h.astype(jnp.bfloat16)
-
-            def fetch(n, ahead_gu):
-                count = tiles * p + n
-                wd_copy(n, lax.rem(count, 2)).wait()
-                for copy in gu_copies(p, n, lax.rem(count, 3)):
-                    copy.wait()
-                if p < 3:
-                    wd_copy(lax.rem(n + 1, tiles), lax.rem(count + 1, 2)).start()
-                else:
-                    pl.when(n < tiles - 1)(lambda: wd_copy(n + 1, lax.rem(count + 1, 2)).start())
-                if ahead_gu:
-                    for copy in gu_copies(p, n + 1, lax.rem(count + 1, 3)):
-                        copy.start()
-
-            fetch(jnp.int32(0), True)
-            product((tiles * p) % 2)
-
-            def later(n, carry):
-                count = tiles * p + n
-                fetch(n, False)
-
-                @pl.when(n < tiles - 1)
-                def _():
-                    for copy in gu_copies(p, n + 1, lax.rem(count + 1, 3)):
-                        copy.start()
-
-                elementwise(n - 1, lax.rem(count - 1, 3))
-                product(lax.rem(count, 2))
                 return carry
 
-            lax.fori_loop(1, tiles, later, 0)
-            if p < 3:
-                for copy in gu_copies(p + 1, 0, (tiles * (p + 1)) % 3):
-                    copy.start()
-            elementwise(tiles - 1, (tiles * (p + 1) - 1) % 3)
+            lax.fori_loop(0, tiles, tile, 0)
             for copy in out_copies(p):
                 copy.start()
+            if p < 3:
+                for copy in gu_copies(p + 1):
+                    copy.start()
 
         def own_x(leg):
-            hold = dyc.at[1, pl.ds(0, rows), :]
-            src, dst = ((x_ref, hold), (hold, xf_ref.at[block(me), :]))[leg]
-            return pltpu.make_async_copy(src, dst, own_sem.at[leg])
+            hold = dgc.at[3, pl.ds(0, rows), :], duc.at[3, pl.ds(0, rows), :]
+            cols = pl.ds(0, ff), pl.ds(ff, ff)
+            return [
+                pltpu.make_async_copy(
+                    *((x_ref.at[:, cols[c]], hold[c]) if leg == 0 else (hold[c], xf_ref.at[block(me), cols[c]])),
+                    own_sem.at[leg, c],
+                )
+                for c in range(2)
+            ]
 
         def own_dy():
-            return pltpu.make_async_copy(dyc.at[0, pl.ds(rows, rows), :], dyf_ref.at[block(me), :], own_sem.at[2])
+            return pltpu.make_async_copy(dyc.at[pl.ds(rows, rows), :], dyf_ref.at[block(me), :], own_sem.at[2, 0])
 
         dys.send(0, 1, 4, 2, 3)
         dy_load(0, 2).start()
         dy_load(0, 3).start()
-        wd_copy(0, 0).start()
-        for copy in gu_copies(0, 0, 0):
+        wd_copy(0).start()
+        for copy in gu_copies(0):
             copy.start()
-        own_x(0).start()
+        for j in range(1, tiles):
+            wd_copy(j).start()
+        for copy in own_x(0):
+            copy.start()
         for copy in w_copies(0, 0):
             copy.start()
         dys.arrived(0)
@@ -269,42 +246,50 @@
         dy_load(0, 1).start()
         act(0)
         own_dy().start()
-        own_x(0).wait()
-        own_x(1).start()
+        for copy in own_x(0):
+            copy.wait()
+        for copy in own_x(1):
+            copy.start()
 
         def first_halves():
             dys.arrived(1, 4)
             dys.send(5, 6, 7, 10)
             xs.send(0, 1, 4, 2, 3)
 
+        def load(p, *numbers):
+            def then():
+                dys.arrived(*numbers)
+                for i in range(4):
+                    dy_load(p, i).start()
+
+            return then
+
+        def load_first():
+            own_dy().wait()
+            for copy in own_x(1):
+                copy.wait()
+            load(1, 7, 10)()
+
         def store_s(sums, _, outs):
             outs[0][...] = sums[0].astype(jnp.bfloat16)
             outs[1][...] = sums[1]
 
-        dx(0, False, [(0, 0, rows), (0, rows, rows)], [], [give_ref.at[0], keep_s_ref], store_s, 4, first_halves)
+        dx(
+            0, False, [(0, 0, rows), (0, rows, rows)], [], [give_ref.at[0], keep_s_ref], store_s,
+            {wtiles - 3: first_halves, wtiles - 1: load_first},
+        )
         pair(0).start()
-        own_x(1).wait()
-        dys.arrived(7, 10)
-        for i in range(4):
-            dy_load(1, i).start()
         act(1)
         dys.arrived(2, 3)
         dys.send(8, 9)
-        give(1, 1)
-        own_dy().wait()
-        dys.arrived(8, 9)
-        for i in range(4):
-            dy_load(2, i).start()
+        give(1, 1, {wtiles - 1: load(2, 8, 9)})
         act(2)
 
         def far_halves():
             dys.arrived(5, 6)
             dys.send(11, 12)
 
-        give(2, 2, 3, far_halves)
-        dys.arrived(11, 12)
-        for i in range(4):
-            dy_load(3, i).start()
+        give(2, 2, {wtiles - 4: far_halves, wtiles - 1: load(3, 11, 12)})
         act(3)
         give(3, 3)
         for copy in out_copies(3):
@@ -312,11 +297,10 @@
 
     pl.run_scoped(
         with_acts,
-        pltpu.VMEM((2, 2 * rows, d), jnp.bfloat16),
-        pltpu.VMEM((2, TILE, d), jnp.bfloat16),
-        pltpu.VMEM((3, 2, 2 * rows, TILE), jnp.bfloat16),
+        pltpu.VMEM((2 * rows, d), jnp.bfloat16),
+        pltpu.VMEM((ff, d), jnp.bfloat16),
+        pltpu.VMEM((2, 2 * rows, ff), jnp.bfloat16),
         pltpu.VMEM((2 * rows, ff), jnp.bfloat16),
-        pltpu.VMEM((2 * rows, TILE), jnp.float32),
     )
 
     xs.arrived(1, 4)
@@ -356,7 +340,7 @@
 
     dx(
         4, True, [(p, rows, rows) for p in (1, 2, 3)], [got_ref.at[p] for p in (1, 2, 3)],
-        [send_x_ref, send_y_ref, keep_n_ref], store_kept, wtiles - 2, far_x,
+        [send_x_ref, send_y_ref, keep_n_ref], store_kept, {wtiles - 2: far_x},
     )
     xs.arrived(0, 7, 8, 9, 10, 11, 12)
     pair(0).wait_recv()
@@ -386,7 +370,7 @@
             pltpu.VMEM((4, 2 * rows, ff), bf16),
             pltpu.VMEM((2, 2, WTILE, ff), bf16),
             dma((2, 13)), dma((2, 13)), dma((4,)), dma((4,)), dma((2, 2)),
-            dma((2, 4)), dma((2,)), dma((3, 2, 4)), dma((3, 4)), dma((3,)),
+            dma((4,)), dma((7,)), dma((2, 4)), dma((3, 4)), dma((3, 2)),
         ],
         compiler_params=pltpu.CompilerParams(
             collective_id=0, has_side_effects=True, vmem_limit_bytes=VMEM_LIMIT
@@ -398,43 +382,71 @@
     )(dy, x, gate, up, wd, wg, wu)
 
 
-def dw_kernel(a_ref, b_hbm, o_ref, b, sems):
-    n = b.shape[1]
-    cuts = [(j * 256, 256) for j in range(n // 256)]
-
-    def load(j):
-        at = pl.ds(cuts[j][0], cuts[j][1])
-        return pltpu.make_async_copy(b_hbm.at[:, at], b.at[:, at], sems.at[j])
-
-    @pl.when(pl.program_id(0) == 0)
+def dw_kernel(a_ref, b_ref, o_ref):
+    o_ref[...] = tn(a_ref[...], b_ref[...]).astype(o_ref.dtype)
+
+
+def dw_kernel_and_move(a_ref, b_ref, src_ref, o_ref, dst_ref, hold, sems):
+    i, steps = pl.program_id(0), pl.num_programs(0)
+    count = hold.shape[1]
+
+    def leg(out, k):
+        at = pl.ds(pl.multiple_of(k * count, count), count)
+        slot = lax.rem(k, 2)
+        pair = (hold.at[slot], dst_ref.at[at, :]) if out else (src_ref.at[at, :], hold.at[slot])
+        return pltpu.make_async_copy(*pair, sems.at[out, slot])
+
+    @pl.when(i > 0)
     def _():
-        for j in range(len(cuts)):
-            load(j).start()
-        for j, (first, count) in enumerate(cuts):
-            load(j).wait()
-            o_ref[:, first : first + count] = tn(a_ref[...], b[:, first : first + count]).astype(o_ref.dtype)
-
-    @pl.when(pl.program_id(0) > 0)
+        leg(0, i - 1).wait()
+        leg(1, i - 1).start()
+
+    @pl.when(i > 1)
     def _():
-        o_ref[...] = tn(a_ref[...], b[...]).astype(o_ref.dtype)
-
-
-def dw(a, b, tm=256):
+        leg(1, i - 2).wait()
+
+    leg(0, i).start()
+    o_ref[...] = tn(a_ref[...], b_ref[...]).astype(o_ref.dtype)
+
+    @pl.when(i == steps - 1)
+    def _():
+        leg(0, i).wait()
+        leg(1, i).start()
+        leg(1, i - 1).wait()
+        leg(1, i).wait()
+
+
+def dw(a, b, moved=None, tm=512):
     tokens, m = a.shape
     n = b.shape[1]
-    return pl.pallas_call(
-        dw_kernel,
-        out_shape=jax.ShapeDtypeStruct((m, n), jnp.bfloat16),
-        grid=(m // tm,),
-        in_specs=[pl.BlockSpec((tokens, tm), lambda i: (0, i)), ANY],
-        out_specs=pl.BlockSpec((tm, n), lambda i: (i, 0)),
-        scratch_shapes=[pltpu.VMEM((tokens, n), jnp.bfloat16), pltpu.SemaphoreType.DMA((n // 256,))],
+    steps = m // tm
+    bf16 = jnp.bfloat16
+    specs = [
+        pl.BlockSpec((tokens, tm), lambda i: (0, i)),
+        pl.BlockSpec((tokens, n), lambda i: (0, 0), pipeline_mode=pl.Buffered(1)),
+    ]
+    out, out_spec = jax.ShapeDtypeStruct((m, n), bf16), pl.BlockSpec((tm, n), lambda i: (i, 0))
+    common = dict(
+        grid=(steps,),
         compiler_params=pltpu.CompilerParams(dimension_semantics=("arbitrary",), vmem_limit_bytes=VMEM_LIMIT),
         cost_estimate=pl.CostEstimate(
             flops=2 * tokens * m * n, bytes_accessed=2 * (tokens * m + tokens * n + m * n), transcendentals=0
         ),
-        name="dw",
-    )(a, b)
+    )
+    if moved is None:
+        return pl.pallas_call(dw_kernel, out_shape=out, in_specs=specs, out_specs=out_spec, name="dw", **common)(a, b)
+    return pl.pallas_call(
+        dw_kernel_and_move,
+        out_shape=[out, jax.ShapeDtypeStruct(moved.shape, bf16)],
+        in_specs=specs + [ANY],
+        out_specs=[out_spec, ANY],
+        scratch_shapes=[
+            pltpu.VMEM((2, moved.shape[0] // steps, moved.shape[1]), bf16),
+            pltpu.SemaphoreType.DMA((2, 2)),
+        ],
+        name="dw_and_move",
+        **common,
+    )(a, b, moved)
 
 
 def solution(mesh):
@@ -448,13 +460,14 @@
         _, xf, dg, du, _, dw_down, _, got, keep_s, keep_n, send_x, send_y = front(dy, x, gate, up, wd, wg, wu)
         from_x = lax.ppermute(send_x, "tp", to_x)
         from_y = lax.ppermute(send_y, "tp", to_y)
-        dw_gate = dw(xf, dg)
+        dw_gate, dw_down = dw(xf, dg, dw_down)
         on_y = (keep_n[half:] + from_x[half:].astype(f32)).astype(bf16)
         on_x = (keep_n[:half] + from_y[half:].astype(f32)).astype(bf16)
         du, on_y, on_x = lax.optimization_barrier((du, on_y, on_x))
         last_y = lax.ppermute(on_y, "tp", to_y)
         last_x = lax.ppermute(on_x, "tp", to_x)
         dw_up = dw(xf, du)
+        keep_s, got, last_y, last_x = lax.optimization_barrier((keep_s, got, last_y, last_x))
         kept = keep_s + got[0].astype(f32)
         dx = jnp.concatenate(
             [

time: 331 us -> 320 us (0.967)
  local copies, waits for them, and re-layouts: 10.6 us -> 0 us
  waiting for transfers between devices: 2.51 us -> 8.7 us
  other arithmetic: 15.6 us -> 12.1 us
    unnamed x1 -> x0, local copies, waits for them, and re-layouts: 10.6 us -> none
    ppermute x1, waiting for transfers between devices: 1.3 us -> 7.49 us  [step(): from_x = lax.ppermute(send_x, 'tp', to_x)]
    pallas_call x2, Pallas kernels: 86.3 us -> 82.1 us  [the longest x1 41.8 us: dw(): pl.pallas_call(dw_kernel_and_move, out_shape=[out, jax.ShapeDtypeStruct(m...]
  transfers between devices with their start and end apart: 4 -> 4, of which waited for: 2 -> 2; matrix products, arithmetic and copies ran while one was open for 2% -> 0% of each run, Pallas kernels for 26% -> 26%
where the time goes in v3:
time: 320 us
  Pallas kernels  295 us (92%)
  other arithmetic  12.1 us (4%)
  waiting for transfers between devices  8.7 us (3%)
  starting transfers between devices  4.11 us (1%)
    pallas_call x1, Pallas kernels, front(): pl.pallas_call(front_kernel, out_shape=[jax.ShapeDtypeStruct(*s) for s in...  212 us
    pallas_call x1, Pallas kernels, dw(): pl.pallas_call(dw_kernel_and_move, out_shape=[out, jax.ShapeDtypeStruct(m...  41.8 us
    pallas_call x1, Pallas kernels, dw(): pl.pallas_call(dw_kernel, out_shape=out, in_specs=specs, out_specs=out_sp...  40.4 us
    ppermute x1, waiting for transfers between devices, step(): from_x = lax.ppermute(send_x, 'tp', to_x)  7.49 us
  transfers between devices with their start and end apart: 4, of which 2 were waited for; matrix products, arithmetic and copies ran while one was open for 0% of the time, Pallas kernels for 26%

profile of v3, /device:TPU:0, one launch (start us, length us, event | category | flops | bytes accessed | tf_op | source)
XLA Modules:
  0.0 320.1 jit_solution(7606416237410810953)
XLA Ops:
  0.6 212.4 %front.1 = (bf16[2560,3584]{1,0:T(8,128)(2,1)}, bf16[2560,3584]{1,0:T(8,128)(2,1)}, bf16[2560,1792]{1,0:T(8,128)(2,1)}, bf16[2560,1792]{1,0:T(8,128)(2,1)}, bf16...) custom-call(bf16[320,3584]{1,0:T(8,128)(2,1)} %dy_ref.1, ...), custom_call_target="tpu_custom_call" | custom-call | flops 131533373440 | bytes 314572800 | tf_op jit(solution)/shard_map/front/pallas_call | solution.py:363
  213.1 1.5 collective-permute-start
  214.6 0.6 collective-permute-start.1
  215.1 41.8 %dw_and_move.1 = (bf16[3584,1792]{1,0:T(8,128)(2,1)}, bf16[1792,3584]{1,0:T(8,128)(2,1)}) custom-call(bf16[2560,3584]{1,0:T(8,128)(2,1)} %get-tuple-element.34.a_ref, bf16[2560,1792]{1,0:T(8,128)(2,1)} %get-tuple-element.35.b_ref, bf16[1792,3584]{1,0:T(8,128)(2,1)} %get-tuple-element.36.src_ref), custom_call_target="tpu_custom_call" | custom-call | flops 32883343360 | bytes 40370176 | tf_op jit(solution)/shard_map/dw_and_move/pallas_call | solution.py:438
  256.9 7.5 %collective-permute-done = bf16[320,3584]{1,0:T(8,128)(2,1)S(1)} collective-permute-done((bf16[320,3584]{1,0:T(8,128)(2,1)}, bf16[320,3584]{1,0:T(8,128)(2,1)S(1)}, u32[]{:S(2)}, u32[]{:S(2)}) %collective-permute-start) | collective-permute-done | bytes 2293792 | tf_op jit(solution)/shard_map/ppermute | solution.py:461
  264.4 1.2 collective-permute-done.1
  265.6 4.2 %add_convert_fusion = (bf16[160,3584]{1,0:T(8,128)(2,1)S(1)}, bf16[160,3584]{1,0:T(8,128)(2,1)}) fusion(f32[320,3584]{1,0:T(8,128)} %get-tuple-element.25, bf16[320,3584]{1,0:T(8,128)(2,1)} %collective-permute-done.1, bf16[320,3584]{1,0:T(8,128)(2,1)S(1)} %collective-permute-done), kind=kLoop, calls=%fused_computation.8 | loop fusion | flops 3440640 | bytes 9175040 | tf_op jit(solution)/shard_map/convert_element_type | solution.py:465
  269.8 1.0 collective-permute-start.2
  270.8 1.1 collective-permute-start.3
  271.8 40.4 %dw.1 = bf16[3584,1792]{1,0:T(8,128)(2,1)} custom-call(bf16[2560,3584]{1,0:T(8,128)(2,1)} %get-tuple-element.34.a_ref, bf16[2560,1792]{1,0:T(8,128)(2,1)} %get-tuple-element.38.b_ref), custom_call_target="tpu_custom_call" | custom-call | flops 32883343360 | bytes 40370176 | tf_op jit(solution)/shard_map/dw/pallas_call | solution.py:437
  312.2 0.0 collective-permute-done.2
  312.2 0.0 collective-permute-done.3
  312.2 3.5 %convert_add_fusion = f32[320,3584]{1,0:T(8,128)S(1)} fusion(f32[320,3584]{1,0:T(8,128)} %get-tuple-element.30, bf16[4,320,3584]{2,1,0:T(8,128)(2,1)} %get-tuple-element.31), kind=kLoop, calls=%fused_computation | loop fusion | flops 2293760 | bytes 11468800 | tf_op jit(solution)/shard_map/add | solution.py:471
  315.8 2.8 fusion.3
  318.6 1.5 pad_maximum_fusion
Async XLA Ops:
  213.1 51.3 %collective-permute-start = (bf16[320,3584]{1,0:T(8,128)(2,1)}, bf16[320,3584]{1,0:T(8,128)(2,1)S(1)}, u32[]{:S(2)}, u32[]{:S(2)}) collective-permute-start(bf16[320,3584]{1,0:T(8,128)(2,1)} %get-tuple-element.26), channel_id=1, source_target_pairs={{0,4},{1,5},{2,6},{3,7},{4,0},{5,1},{6,2},{7,3}} | collective-permute-start | bytes 6881288 | tf_op jit(solution)/shard_map/ppermute | solution.py:461
  214.6 51.0 %collective-permute-start.1 = (bf16[320,3584]{1,0:T(8,128)(2,1)}, bf16[320,3584]{1,0:T(8,128)(2,1)}, u32[]{:S(2)}, u32[]{:S(2)}) collective-permute-start(bf16[320,3584]{1,0:T(8,128)(2,1)} %get-tuple-element.27), channel_id=1, source_target_pairs={{0,2},{1,3},{2,0},{3,1},{4,6},{5,7},{6,4},{7,5}} | collective-permute-start | bytes 6881288 | tf_op jit(solution)/shard_map/ppermute | solution.py:462
  269.8 42.4 %collective-permute-start.2 = (bf16[160,3584]{1,0:T(8,128)(2,1)}, bf16[160,3584]{1,0:T(8,128)(2,1)}, u32[]{:S(2)}, u32[]{:S(2)}) collective-permute-start(bf16[160,3584]{1,0:T(8,128)(2,1)} %get-tuple-element.28), channel_id=1, source_target_pairs={{0,2},{1,3},{2,0},{3,1},{4,6},{5,7},{6,4},{7,5}} | collective-permute-start | bytes 3440648 | tf_op jit(solution)/shard_map/ppermute | solution.py:467
  270.8 41.5 %collective-permute-start.3 = (bf16[160,3584]{1,0:T(8,128)(2,1)S(1)}, bf16[160,3584]{1,0:T(8,128)(2,1)}, u32[]{:S(2)}, u32[]{:S(2)}) collective-permute-start(bf16[160,3584]{1,0:T(8,128)(2,1)S(1)} %get-tuple-element.29), channel_id=1, source_target_pairs={{0,4},{1,5},{2,6},{3,7},{4,0},{5,1},{6,2},{7,3}} | collective-permute-start | bytes 3440648 | tf_op jit(solution)/shard_map/ppermute | solution.py:468

commit v4 on v3

--- a/solution.py
+++ b/solution.py
@@ -36,7 +36,7 @@
 
 def front_kernel(
     dy_ref, x_ref, gate_ref, up_ref, wd_ref, wg_ref, wu_ref,
-    dyf_ref, xf_ref, dg_ref, du_ref, h_ref, dwd_ref, give_ref, got_ref, keep_s_ref, keep_n_ref, send_x_ref, send_y_ref,
+    dyf_ref, xf_ref, dg_ref, du_ref, h_ref, give_ref, got_ref, keep_s_ref, keep_n_ref, send_x_ref, send_y_ref,
     dgc, duc, wbuf, send_sem, recv_sem, pair_send, pair_recv, w_sem, dy_sem, wd_sem, gu_sem, out_sem, own_sem,
 ):
     rows, d = dy_ref.shape
@@ -126,7 +126,7 @@
             pltpu.make_async_copy(ref.at[at, :], wbuf.at[slot, i], w_sem.at[slot, i]) for i, ref in enumerate((wg_ref, wu_ref))
         ]
 
-    def dx(k, last, parts, ins, outs, store, hooks):
+    def dx(k, last, parts, ins, outs, store, hooks, heights=None):
         def body(step, *refs):
             n = step.index[0]
             slot = lax.rem(wtiles * k + n, 2)
@@ -149,9 +149,15 @@
             ]
             store(sums, refs[: len(ins)], refs[len(ins) :])
 
-        spec = pl.BlockSpec((rows, WTILE), lambda n: (0, n))
+        def spec(height):
+            return pl.BlockSpec((height, WTILE), lambda n: (0, n))
+
         pltpu.emit_pipeline(
-            body, grid=(wtiles,), in_specs=[spec] * len(ins), out_specs=[spec] * len(outs), _explicit_indices=True
+            body,
+            grid=(wtiles,),
+            in_specs=[spec(rows) for _ in ins],
+            out_specs=[spec(height) for height in heights or [rows] * len(outs)],
+            _explicit_indices=True,
         )(*ins, *outs)
 
     def give(k, p, hooks={}):
@@ -235,15 +241,16 @@
         wd_copy(0).start()
         for copy in gu_copies(0):
             copy.start()
-        for j in range(1, tiles):
+        wd_copy(1).start()
+        dys.arrived(0)
+        dy_load(0, 0).start()
+        dy_load(0, 1).start()
+        for j in range(2, tiles):
             wd_copy(j).start()
         for copy in own_x(0):
             copy.start()
         for copy in w_copies(0, 0):
             copy.start()
-        dys.arrived(0)
-        dy_load(0, 0).start()
-        dy_load(0, 1).start()
         act(0)
         own_dy().start()
         for copy in own_x(0):
@@ -305,43 +312,34 @@
 
     xs.arrived(1, 4)
     xs.send(5, 6, 7, 10)
-
-    def down(h_tile, dy_tile, o_ref):
-        o_ref[...] = tn(h_tile[...], dy_tile[...]).astype(jnp.bfloat16)
-
-    tokens = dyf_ref.shape[0]
-    pltpu.emit_pipeline(
-        down,
-        grid=(ff // 896, d // 512),
-        in_specs=[
-            pl.BlockSpec((tokens, 896), lambda i, j: (0, i)),
-            pl.BlockSpec((tokens, 512), lambda i, j: (0, j)),
-        ],
-        out_specs=[pl.BlockSpec((896, 512), lambda i, j: (i, j))],
-    )(h_ref, dyf_ref, dwd_ref)
-
-    xs.arrived(2, 3)
-    xs.send(8, 9)
-    for p in (1, 2, 3):
+    for p in (1, 2):
         pair(p).wait_recv()
 
-    def store_kept(sums, gots, outs):
-        near0, near1, far_sum = (s + g[...].astype(jnp.float32) for s, g in zip(sums, gots))
+    def second_halves():
+        xs.arrived(2, 3)
+        xs.send(8, 9)
+
+    def store_near(sums, gots, outs):
+        near0, near1 = (s + g[...].astype(jnp.float32) for s, g in zip(sums, gots))
         to_x, to_y, kept = outs
-        to_x[pl.ds(0, half), :] = near0[:half].astype(jnp.bfloat16)
-        to_y[pl.ds(0, half), :] = near0[half:].astype(jnp.bfloat16)
+        to_x[...] = near0[:half].astype(jnp.bfloat16)
+        to_y[...] = near0[half:].astype(jnp.bfloat16)
         kept[...] = near1
-        to_x[pl.ds(half, half), :] = far_sum[:half].astype(jnp.bfloat16)
-        to_y[pl.ds(half, half), :] = far_sum[half:].astype(jnp.bfloat16)
-
-    def far_x():
-        xs.arrived(5, 6)
-        xs.send(11, 12)
 
     dx(
-        4, True, [(p, rows, rows) for p in (1, 2, 3)], [got_ref.at[p] for p in (1, 2, 3)],
-        [send_x_ref, send_y_ref, keep_n_ref], store_kept, {wtiles - 2: far_x},
+        4, False, [(p, rows, rows) for p in (1, 2)], [got_ref.at[1], got_ref.at[2]],
+        [send_x_ref.at[0], send_y_ref.at[0], keep_n_ref], store_near, {wtiles - 2: second_halves}, [half, half, rows],
     )
+    pair(3).wait_recv()
+
+    def store_far(sums, gots, outs):
+        total = sums[0] + gots[0][...].astype(jnp.float32)
+        outs[0][...] = total[:half].astype(jnp.bfloat16)
+        outs[1][...] = total[half:].astype(jnp.bfloat16)
+
+    dx(5, True, [(3, rows, rows)], [got_ref.at[3]], [send_x_ref.at[1], send_y_ref.at[1]], store_far, {}, [half, half])
+    xs.arrived(5, 6)
+    xs.send(11, 12)
     xs.arrived(0, 7, 8, 9, 10, 11, 12)
     pair(0).wait_recv()
     for p in range(4):
@@ -356,8 +354,8 @@
     bf16, f32 = jnp.bfloat16, jnp.float32
     shapes = [
         ((tokens, d), bf16), ((tokens, d), bf16), ((tokens, ff), bf16), ((tokens, ff), bf16), ((tokens, ff), bf16),
-        ((ff, d), bf16), ((4, rows, d), bf16), ((4, rows, d), bf16), ((rows, d), f32), ((rows, d), f32),
-        ((rows, d), bf16), ((rows, d), bf16),
+        ((4, rows, d), bf16), ((4, rows, d), bf16), ((rows, d), f32), ((rows, d), f32),
+        ((2, rows // 2, d), bf16), ((2, rows // 2, d), bf16),
     ]
     dma = pltpu.SemaphoreType.DMA
     return pl.pallas_call(
@@ -376,7 +374,7 @@
             collective_id=0, has_side_effects=True, vmem_limit_bytes=VMEM_LIMIT
         ),
         cost_estimate=pl.CostEstimate(
-            flops=8 * tokens * d * ff, bytes_accessed=300 * 2**20, transcendentals=tokens * ff
+            flops=6 * tokens * d * ff, bytes_accessed=300 * 2**20, transcendentals=tokens * ff
         ),
         name="front",
     )(dy, x, gate, up, wd, wg, wu)
@@ -386,67 +384,103 @@
     o_ref[...] = tn(a_ref[...], b_ref[...]).astype(o_ref.dtype)
 
 
-def dw_kernel_and_move(a_ref, b_ref, src_ref, o_ref, dst_ref, hold, sems):
-    i, steps = pl.program_id(0), pl.num_programs(0)
-    count = hold.shape[1]
-
-    def leg(out, k):
-        at = pl.ds(pl.multiple_of(k * count, count), count)
-        slot = lax.rem(k, 2)
-        pair = (hold.at[slot], dst_ref.at[at, :]) if out else (src_ref.at[at, :], hold.at[slot])
-        return pltpu.make_async_copy(*pair, sems.at[out, slot])
-
-    @pl.when(i > 0)
-    def _():
-        leg(0, i - 1).wait()
-        leg(1, i - 1).start()
-
-    @pl.when(i > 1)
-    def _():
-        leg(1, i - 2).wait()
-
-    leg(0, i).start()
-    o_ref[...] = tn(a_ref[...], b_ref[...]).astype(o_ref.dtype)
-
-    @pl.when(i == steps - 1)
-    def _():
-        leg(0, i).wait()
-        leg(1, i).start()
-        leg(1, i - 1).wait()
-        leg(1, i).wait()
-
-
-def dw(a, b, moved=None, tm=512):
+def dw(a, b, tm=512):
     tokens, m = a.shape
     n = b.shape[1]
-    steps = m // tm
-    bf16 = jnp.bfloat16
-    specs = [
-        pl.BlockSpec((tokens, tm), lambda i: (0, i)),
-        pl.BlockSpec((tokens, n), lambda i: (0, 0), pipeline_mode=pl.Buffered(1)),
-    ]
-    out, out_spec = jax.ShapeDtypeStruct((m, n), bf16), pl.BlockSpec((tm, n), lambda i: (i, 0))
-    common = dict(
-        grid=(steps,),
+    return pl.pallas_call(
+        dw_kernel,
+        out_shape=jax.ShapeDtypeStruct((m, n), jnp.bfloat16),
+        grid=(m // tm,),
+        in_specs=[
+            pl.BlockSpec((tokens, tm), lambda i: (0, i)),
+            pl.BlockSpec((tokens, n), lambda i: (0, 0), pipeline_mode=pl.Buffered(1)),
+        ],
+        out_specs=pl.BlockSpec((tm, n), lambda i: (i, 0)),
         compiler_params=pltpu.CompilerParams(dimension_semantics=("arbitrary",), vmem_limit_bytes=VMEM_LIMIT),
         cost_estimate=pl.CostEstimate(
             flops=2 * tokens * m * n, bytes_accessed=2 * (tokens * m + tokens * n + m * n), transcendentals=0
         ),
-    )
-    if moved is None:
-        return pl.pallas_call(dw_kernel, out_shape=out, in_specs=specs, out_specs=out_spec, name="dw", **common)(a, b)
+        name="dw",
+    )(a, b)
+
+
+def dw_two(h, dy, x, dg, tile=512):
+    tokens, ff = h.shape
+    d = dy.shape[1]
+    steps = d // tile
+
+    def kernel(h_ref, dy_ref, x_ref, dg_hbm, down_ref, gate_ref, held, sem):
+        i = pl.program_id(0)
+        load = pltpu.make_async_copy(dg_hbm, held, sem)
+
+        @pl.when(i == 0)
+        def _():
+            load.start()
+
+        @pl.when(i < steps)
+        def _():
+            down_ref[...] = tn(h_ref[...], dy_ref[...]).astype(down_ref.dtype)
+
+        @pl.when(i == steps - 1)
+        def _():
+            load.wait()
+
+        @pl.when(i >= steps)
+        def _():
+            gate_ref[...] = tn(x_ref[...], held[...]).astype(gate_ref.dtype)
+
+    def first(i):
+        return jnp.minimum(i, steps - 1)
+
+    def second(i):
+        return jnp.maximum(i - steps, 0)
+
     return pl.pallas_call(
-        dw_kernel_and_move,
-        out_shape=[out, jax.ShapeDtypeStruct(moved.shape, bf16)],
-        in_specs=specs + [ANY],
-        out_specs=[out_spec, ANY],
-        scratch_shapes=[
-            pltpu.VMEM((2, moved.shape[0] // steps, moved.shape[1]), bf16),
-            pltpu.SemaphoreType.DMA((2, 2)),
+        kernel,
+        out_shape=[jax.ShapeDtypeStruct((ff, d), jnp.bfloat16), jax.ShapeDtypeStruct((d, ff), jnp.bfloat16)],
+        grid=(2 * steps,),
+        in_specs=[
+            pl.BlockSpec((tokens, ff), lambda i: (0, 0), pipeline_mode=pl.Buffered(1)),
+            pl.BlockSpec((tokens, tile), lambda i: (0, first(i))),
+            pl.BlockSpec((tokens, tile), lambda i: (0, second(i))),
+            ANY,
         ],
-        name="dw_and_move",
-        **common,
-    )(a, b, moved)
+        out_specs=[
+            pl.BlockSpec((ff, tile), lambda i: (0, first(i))),
+            pl.BlockSpec((tile, ff), lambda i: (second(i), 0)),
+        ],
+        scratch_shapes=[pltpu.VMEM((tokens, ff), jnp.bfloat16), pltpu.SemaphoreType.DMA(())],
+        compiler_params=pltpu.CompilerParams(dimension_semantics=("arbitrary",), vmem_limit_bytes=VMEM_LIMIT),
+        cost_estimate=pl.CostEstimate(
+            flops=4 * tokens * d * ff, bytes_accessed=4 * (tokens * d + tokens * ff + d * ff), transcendentals=0
+        ),
+        name="dw_two",
+    )(h, dy, x, dg)
+
+
+def sum_rows(kept, got, from_x, from_y, last_x, last_y, tile=896):
+    rows, d = kept.shape
+    half = rows // 2
+
+    def kernel(kept_ref, got_ref, fx_ref, fy_ref, lx_ref, ly_ref, o_ref):
+        f32 = jnp.float32
+        for at, near, last in ((pl.ds(0, half), fx_ref, ly_ref), (pl.ds(half, half), fy_ref, lx_ref)):
+            total = kept_ref[at, :] + got_ref[0, at, :].astype(f32) + near[0].astype(f32) + last[...].astype(f32)
+            o_ref[at, :] = total.astype(o_ref.dtype)
+
+    full = pl.BlockSpec((rows, tile), lambda i: (0, i))
+    part = pl.BlockSpec((1, half, tile), lambda i: (0, 0, i))
+    last = pl.BlockSpec((half, tile), lambda i: (0, i))
+    return pl.pallas_call(
+        kernel,
+        out_shape=jax.ShapeDtypeStruct((rows, d), jnp.bfloat16),
+        grid=(d // tile,),
+        in_specs=[full, pl.BlockSpec((1, rows, tile), lambda i: (0, 0, i)), part, part, last, last],
+        out_specs=full,
+        compiler_params=pltpu.CompilerParams(dimension_semantics=("arbitrary",), vmem_limit_bytes=VMEM_LIMIT),
+        cost_estimate=pl.CostEstimate(flops=4 * rows * d, bytes_accessed=14 * rows * d, transcendentals=0),
+        name="sum_rows",
+    )(kept, got, from_x, from_y, last_x, last_y)
 
 
 def solution(mesh):
@@ -457,24 +491,17 @@
     def step(x, dy, gate, up, wg, wu, wd):
         bf16, f32 = jnp.bfloat16, jnp.float32
         half = x.shape[0] // 2
-        _, xf, dg, du, _, dw_down, _, got, keep_s, keep_n, send_x, send_y = front(dy, x, gate, up, wd, wg, wu)
+        dyf, xf, dg, du, h, _, got, keep_s, keep_n, send_x, send_y = front(dy, x, gate, up, wd, wg, wu)
         from_x = lax.ppermute(send_x, "tp", to_x)
         from_y = lax.ppermute(send_y, "tp", to_y)
-        dw_gate, dw_down = dw(xf, dg, dw_down)
-        on_y = (keep_n[half:] + from_x[half:].astype(f32)).astype(bf16)
-        on_x = (keep_n[:half] + from_y[half:].astype(f32)).astype(bf16)
+        dw_down, dw_gate = dw_two(h, dyf, xf, dg)
+        on_y = (keep_n[half:] + from_x[1].astype(f32)).astype(bf16)
+        on_x = (keep_n[:half] + from_y[1].astype(f32)).astype(bf16)
         du, on_y, on_x = lax.optimization_barrier((du, on_y, on_x))
         last_y = lax.ppermute(on_y, "tp", to_y)
         last_x = lax.ppermute(on_x, "tp", to_x)
         dw_up = dw(xf, du)
-        keep_s, got, last_y, last_x = lax.optimization_barrier((keep_s, got, last_y, last_x))
-        kept = keep_s + got[0].astype(f32)
-        dx = jnp.concatenate(
-            [
-                kept[:half] + from_x[:half].astype(f32) + last_y.astype(f32),
-                kept[half:] + from_y[:half].astype(f32) + last_x.astype(f32),
-            ]
-        ).astype(bf16)
+        dx = sum_rows(keep_s, got, from_x, from_y, last_x, last_y)
         return dx, dw_gate, dw_up, dw_down
 
     rows, cols, down = P(("dp", "tp"), None), P("dp", "tp"), P("tp", None)

time: 320 us -> 314 us (0.981)
  waiting for transfers between devices: 8.7 us -> 0.01 us
  other arithmetic: 12.1 us -> 5.02 us
  Pallas kernels: 295 us -> 302 us
    pallas_call x2 -> x3, Pallas kernels: 82.1 us -> 124 us  [the longest x1 77.1 us: dw_two(): pl.pallas_call(kernel, out_shape=[jax.ShapeDtypeStruct((ff, d), jnp.bfloa...]
    pallas_call x1, Pallas kernels: 212 us -> 179 us  [front(): pl.pallas_call(front_kernel, out_shape=[jax.ShapeDtypeStruct(*s) for s in...]
    ppermute x1, waiting for transfers between devices: 7.49 us -> 0.01 us  [step(): from_x = lax.ppermute(send_x, 'tp', to_x)]
    add x1 -> x0, other arithmetic: 3.54 us -> none  [step(): kept = keep_s + got[0].astype(f32)]
  transfers between devices with their start and end apart: 4 -> 4, of which waited for: 2 -> 0; matrix products, arithmetic and copies ran while one was open for 0% -> 0% of each run, Pallas kernels for 26% -> 37%
where the time goes in v4:
time: 314 us
  Pallas kernels  302 us (96%)
  other arithmetic  5.02 us (2%)
  starting transfers between devices  4.07 us (1%)
    pallas_call x1, Pallas kernels, front(): pl.pallas_call(front_kernel, out_shape=[jax.ShapeDtypeStruct(*s) for s in...  179 us
    pallas_call x1, Pallas kernels, dw_two(): pl.pallas_call(kernel, out_shape=[jax.ShapeDtypeStruct((ff, d), jnp.bfloa...  77.1 us
    pallas_call x1, Pallas kernels, dw(): pl.pallas_call(dw_kernel, out_shape=jax.ShapeDtypeStruct((m, n), jnp.bflo...  40.4 us
  transfers between devices with their start and end apart: 4, of which 0 were waited for; matrix products, arithmetic and copies ran while one was open for 0% of the time, Pallas kernels for 37%

profile of v4, /device:TPU:0, one launch (start us, length us, event | category | flops | bytes accessed | tf_op | source)
XLA Modules:
  0.0 313.8 jit_solution(11173994633397877410)
XLA Ops:
  0.6 178.8 %front.1 = (bf16[2560,3584]{1,0:T(8,128)(2,1)}, bf16[2560,3584]{1,0:T(8,128)(2,1)}, bf16[2560,1792]{1,0:T(8,128)(2,1)}, bf16[2560,1792]{1,0:T(8,128)(2,1)}, bf16...) custom-call(bf16[320,3584]{1,0:T(8,128)(2,1)} %dy_ref.1, ...), custom_call_target="tpu_custom_call" | custom-call | flops 98650030080 | bytes 314572800 | tf_op jit(solution)/shard_map/front/pallas_call | solution.py:361
  179.4 1.5 collective-permute-start
  180.9 0.5 collective-permute-start.1
  181.5 77.1 %dw_two.1 = (bf16[1792,3584]{1,0:T(8,128)(2,1)}, bf16[3584,1792]{1,0:T(8,128)(2,1)}) custom-call(bf16[2560,1792]{1,0:T(8,128)(2,1)} %get-tuple-element.27.h_ref, bf16[2560,3584]{1,0:T(8,128)(2,1)} %get-tuple-element.28.dy_ref, bf16[2560,3584]{1,0:T(8,128)(2,1)} %get-tuple-element.29.x_ref.a_ref, bf16[2560,1792]{1,0:T(8,128)(2,1)} %get-tuple-element.30.dg_hbm), custom_call_target="tpu_custom_call" | custom-call | flops 65766686720 | bytes 80740352 | tf_op jit(solution)/shard_map/dw_two/pallas_call | solution.py:438
  258.6 0.0 collective-permute-done.fx_ref
  258.6 0.0 copy-start
  258.6 0.0 collective-permute-done.1.fy_ref
  258.6 5.0 %fusion = (bf16[160,3584]{1,0:T(8,128)(2,1)}, bf16[160,3584]{1,0:T(8,128)(2,1)S(1)}) fusion(f32[320,3584]{1,0:T(8,128)} %get-tuple-element.24, bf16[2,160,3584]{2,1,0:T(8,128)(2,1)} %collective-permute-done.1.fy_ref, bf16[2,160,3584]{2,1,0:T(8,128)(2,1)S(1)} %collective-permute-done.fx_ref), kind=kLoop, calls=%fused_computation.1 | loop fusion | flops 3440640 | bytes 9175040 | tf_op jit(solution)/shard_map/convert_element_type | solution.py:499
  263.7 0.0 copy-done
  263.7 1.5 collective-permute-start.2
  265.2 0.5 collective-permute-start.3
  265.7 40.4 %dw.1 = bf16[3584,1792]{1,0:T(8,128)(2,1)} custom-call(bf16[2560,3584]{1,0:T(8,128)(2,1)} %get-tuple-element.29.x_ref.a_ref, bf16[2560,1792]{1,0:T(8,128)(2,1)} %get-tuple-element.32.b_ref), custom_call_target="tpu_custom_call" | custom-call | flops 32883343360 | bytes 40370176 | tf_op jit(solution)/shard_map/dw/pallas_call | solution.py:390
  306.1 0.0 collective-permute-done.2.lx_ref
  306.1 0.0 copy-start.1
  306.1 0.0 collective-permute-done.3.ly_ref
  306.1 0.0 copy-start.2
  306.1 1.0 copy-done.1
  307.1 0.5 copy-done.2
  307.6 6.2 %sum_rows.1 = bf16[320,3584]{1,0:T(8,128)(2,1)} custom-call(f32[320,3584]{1,0:T(8,128)} %get-tuple-element.19.kept_ref, bf16[4,320,3584]{2,1,0:T(8,128)(2,1)} %get-tuple-element.20.got_ref, bf16[2,160,3584]{2,1,0:T(8,128)(2,1)} %copy-done, bf16[2,160,3584]{2,1,0:T(8,128)(2,1)} %collective-permute-done.1.fy_ref, bf16[160,3584]{1,0:T(8,128)(2,1)} %copy-done.1, ...), custom_call_target="tpu_custom_call" | custom-call | flops 4587520 | bytes 16056320 | tf_op jit(solution)/shard_map/sum_rows/pallas_call | solution.py:474
Async XLA Ops:
  179.4 79.2 %collective-permute-start = (bf16[2,160,3584]{2,1,0:T(8,128)(2,1)}, bf16[2,160,3584]{2,1,0:T(8,128)(2,1)S(1)}, u32[]{:S(2)}, u32[]{:S(2)}) collective-permute-start(bf16[2,160,3584]{2,1,0:T(8,128)(2,1)} %get-tuple-element.21), channel_id=1, source_target_pairs={{0,4},{1,5},{2,6},{3,7},{4,0},{5,1},{6,2},{7,3}} | collective-permute-start | bytes 6881288 | tf_op jit(solution)/shard_map/ppermute | solution.py:495
  180.9 77.7 %collective-permute-start.1 = (bf16[2,160,3584]{2,1,0:T(8,128)(2,1)}, bf16[2,160,3584]{2,1,0:T(8,128)(2,1)}, u32[]{:S(2)}, u32[]{:S(2)}) collective-permute-start(bf16[2,160,3584]{2,1,0:T(8,128)(2,1)} %get-tuple-element.22), channel_id=1, source_target_pairs={{0,2},{1,3},{2,0},{3,1},{4,6},{5,7},{6,4},{7,5}} | collective-permute-start | bytes 6881288 | tf_op jit(solution)/shard_map/ppermute | solution.py:496
  258.6 5.0 %copy-start = (bf16[2,160,3584]{2,1,0:T(8,128)(2,1)}, bf16[2,160,3584]{2,1,0:T(8,128)(2,1)S(1)}, u32[]{:S(2)}) copy-start(bf16[2,160,3584]{2,1,0:T(8,128)(2,1)S(1)} %collective-permute-done.fx_ref) | copy-start | bytes 6881284
  263.7 42.4 %collective-permute-start.2 = (bf16[160,3584]{1,0:T(8,128)(2,1)}, bf16[160,3584]{1,0:T(8,128)(2,1)S(1)}, u32[]{:S(2)}, u32[]{:S(2)}) collective-permute-start(bf16[160,3584]{1,0:T(8,128)(2,1)} %get-tuple-element.25), channel_id=1, source_target_pairs={{0,4},{1,5},{2,6},{3,7},{4,0},{5,1},{6,2},{7,3}} | collective-permute-start | bytes 3440648 | tf_op jit(solution)/shard_map/ppermute | solution.py:502
  265.2 40.9 %collective-permute-start.3 = (bf16[160,3584]{1,0:T(8,128)(2,1)S(1)}, bf16[160,3584]{1,0:T(8,128)(2,1)S(1)}, u32[]{:S(2)}, u32[]{:S(2)}) collective-permute-start(bf16[160,3584]{1,0:T(8,128)(2,1)S(1)} %get-tuple-element.26), channel_id=1, source_target_pairs={{0,2},{1,3},{2,0},{3,1},{4,6},{5,7},{6,4},{7,5}} | collective-permute-start | bytes 3440648 | tf_op jit(solution)/shard_map/ppermute | solution.py:501
  306.1 1.0 copy-start.1
  306.1 1.5 copy-start.2

commit v5 on v4

--- a/solution.py
+++ b/solution.py
@@ -298,7 +298,12 @@
 
         give(2, 2, {wtiles - 4: far_halves, wtiles - 1: load(3, 11, 12)})
         act(3)
-        give(3, 3)
+
+        def first_x_halves():
+            xs.arrived(1, 4)
+            xs.send(5, 6, 7, 10)
+
+        give(3, 3, {0: first_x_halves})
         for copy in out_copies(3):
             copy.wait()
 
@@ -310,8 +315,6 @@
         pltpu.VMEM((2 * rows, ff), jnp.bfloat16),
     )
 
-    xs.arrived(1, 4)
-    xs.send(5, 6, 7, 10)
     for p in (1, 2):
         pair(p).wait_recv()
 
@@ -328,7 +331,7 @@
 
     dx(
         4, False, [(p, rows, rows) for p in (1, 2)], [got_ref.at[1], got_ref.at[2]],
-        [send_x_ref.at[0], send_y_ref.at[0], keep_n_ref], store_near, {wtiles - 2: second_halves}, [half, half, rows],
+        [send_x_ref.at[0], send_y_ref.at[0], keep_n_ref], store_near, {0: second_halves}, [half, half, rows],
     )
     pair(3).wait_recv()
 
@@ -458,6 +461,28 @@
     )(h, dy, x, dg)
 
 
+def sum_on(kept, from_x, from_y, tile=1792):
+    rows, d = kept.shape
+    half = rows // 2
+
+    def kernel(kept_ref, fx_ref, fy_ref, ony_ref, onx_ref):
+        onx_ref[...] = (kept_ref[pl.ds(0, half), :] + fy_ref[0].astype(jnp.float32)).astype(jnp.bfloat16)
+        ony_ref[...] = (kept_ref[pl.ds(half, half), :] + fx_ref[0].astype(jnp.float32)).astype(jnp.bfloat16)
+
+    part = pl.BlockSpec((1, half, tile), lambda i: (1, 0, i))
+    out = pl.BlockSpec((half, tile), lambda i: (0, i))
+    return pl.pallas_call(
+        kernel,
+        out_shape=[jax.ShapeDtypeStruct((half, d), jnp.bfloat16)] * 2,
+        grid=(d // tile,),
+        in_specs=[pl.BlockSpec((rows, tile), lambda i: (0, i)), part, part],
+        out_specs=[out, out],
+        compiler_params=pltpu.CompilerParams(dimension_semantics=("arbitrary",), vmem_limit_bytes=VMEM_LIMIT),
+        cost_estimate=pl.CostEstimate(flops=rows * d, bytes_accessed=8 * rows * d, transcendentals=0),
+        name="sum_on",
+    )(kept, from_x, from_y)
+
+
 def sum_rows(kept, got, from_x, from_y, last_x, last_y, tile=896):
     rows, d = kept.shape
     half = rows // 2
@@ -489,14 +514,11 @@
     to_y = [(i, i ^ 2) for i in range(devices)]
 
     def step(x, dy, gate, up, wg, wu, wd):
-        bf16, f32 = jnp.bfloat16, jnp.float32
-        half = x.shape[0] // 2
         dyf, xf, dg, du, h, _, got, keep_s, keep_n, send_x, send_y = front(dy, x, gate, up, wd, wg, wu)
         from_x = lax.ppermute(send_x, "tp", to_x)
         from_y = lax.ppermute(send_y, "tp", to_y)
         dw_down, dw_gate = dw_two(h, dyf, xf, dg)
-        on_y = (keep_n[half:] + from_x[1].astype(f32)).astype(bf16)
-        on_x = (keep_n[:half] + from_y[1].astype(f32)).astype(bf16)
+        on_y, on_x = sum_on(keep_n, from_x, from_y)
         du, on_y, on_x = lax.optimization_barrier((du, on_y, on_x))
         last_y = lax.ppermute(on_y, "tp", to_y)
         last_x = lax.ppermute(on_x, "tp", to_x)

time: 314 us -> 314 us (level)
  other arithmetic: 5.02 us -> 0 us
  Pallas kernels: 302 us -> 307 us
    convert_element_type x1 -> x0, other arithmetic: 5.02 us -> none  [step(): on_x = (keep_n[:half] + from_y[1].astype(f32)).astype(bf16)]
    pallas_call x0 -> x1, Pallas kernels: none -> 4.08 us  [sum_on(): pl.pallas_call(kernel, out_shape=[jax.ShapeDtypeStruct((half, d), jnp.bfl...]
where the time goes in v5:
time: 314 us
  Pallas kernels  307 us (98%)
  starting transfers between devices  4.07 us (1%)
    pallas_call x1, Pallas kernels, front(): pl.pallas_call(front_kernel, out_shape=[jax.ShapeDtypeStruct(*s) for s in...  179 us
    pallas_call x1, Pallas kernels, dw_two(): pl.pallas_call(kernel, out_shape=[jax.ShapeDtypeStruct((ff, d), jnp.bfloa...  77.1 us
    pallas_call x1, Pallas kernels, dw(): pl.pallas_call(dw_kernel, out_shape=jax.ShapeDtypeStruct((m, n), jnp.bflo...  40.4 us
  transfers between devices with their start and end apart: 4, of which 0 were waited for; matrix products, arithmetic and copies ran while one was open for 0% of the time, Pallas kernels for 37%

profile of v5, /device:TPU:0, one launch (start us, length us, event | category | flops | bytes accessed | tf_op | source)
XLA Modules:
  0.0 314.1 jit_solution(4868778204142365933)
XLA Ops:
  0.6 178.8 %front.1 = (bf16[2560,3584]{1,0:T(8,128)(2,1)}, bf16[2560,3584]{1,0:T(8,128)(2,1)}, bf16[2560,1792]{1,0:T(8,128)(2,1)}, bf16[2560,1792]{1,0:T(8,128)(2,1)}, bf16...) custom-call(bf16[320,3584]{1,0:T(8,128)(2,1)} %dy_ref.1, ...), custom_call_target="tpu_custom_call" | custom-call | flops 98650030080 | bytes 314572800 | tf_op jit(solution)/shard_map/front/pallas_call | solution.py:364
  179.4 1.5 collective-permute-start
  180.9 0.5 collective-permute-start.1
  181.4 77.1 %dw_two.1 = (bf16[1792,3584]{1,0:T(8,128)(2,1)}, bf16[3584,1792]{1,0:T(8,128)(2,1)}) custom-call(bf16[2560,1792]{1,0:T(8,128)(2,1)} %get-tuple-element.31.h_ref, bf16[2560,3584]{1,0:T(8,128)(2,1)} %get-tuple-element.32.dy_ref, bf16[2560,3584]{1,0:T(8,128)(2,1)} %get-tuple-element.33.x_ref.a_ref, bf16[2560,1792]{1,0:T(8,128)(2,1)} %get-tuple-element.34.dg_hbm), custom_call_target="tpu_custom_call" | custom-call | flops 65766686720 | bytes 80740352 | tf_op jit(solution)/shard_map/dw_two/pallas_call | solution.py:441
  258.6 0.0 collective-permute-done.fx_ref
  258.6 0.0 copy-start
  258.6 0.0 collective-permute-done.1.fy_ref
  258.6 1.4 copy-done
  260.0 4.1 %sum_on.1 = (bf16[160,3584]{1,0:T(8,128)(2,1)}, bf16[160,3584]{1,0:T(8,128)(2,1)}) custom-call(f32[320,3584]{1,0:T(8,128)} %get-tuple-element.26.kept_ref, bf16[2,160,3584]{2,1,0:T(8,128)(2,1)} %copy-done, bf16[2,160,3584]{2,1,0:T(8,128)(2,1)} %collective-permute-done.1.fy_ref), custom_call_target="tpu_custom_call" | custom-call | flops 1146880 | bytes 9175040 | tf_op jit(solution)/shard_map/sum_on/pallas_call | solution.py:474
  264.0 1.5 collective-permute-start.2
  265.5 0.5 collective-permute-start.3
  266.1 40.4 %dw.1 = bf16[3584,1792]{1,0:T(8,128)(2,1)} custom-call(bf16[2560,3584]{1,0:T(8,128)(2,1)} %get-tuple-element.33.x_ref.a_ref, bf16[2560,1792]{1,0:T(8,128)(2,1)} %get-tuple-element.36.b_ref), custom_call_target="tpu_custom_call" | custom-call | flops 32883343360 | bytes 40370176 | tf_op jit(solution)/shard_map/dw/pallas_call | solution.py:393
  306.4 0.0 collective-permute-done.2.lx_ref
  306.4 0.0 copy-start.1
  306.4 0.0 collective-permute-done.3.ly_ref
  306.4 0.0 copy-start.2
  306.4 1.0 copy-done.1
  307.5 0.5 copy-done.2
  307.9 6.2 %sum_rows.1 = bf16[320,3584]{1,0:T(8,128)(2,1)} custom-call(f32[320,3584]{1,0:T(8,128)} %get-tuple-element.21.kept_ref, bf16[4,320,3584]{2,1,0:T(8,128)(2,1)} %get-tuple-element.22.got_ref, bf16[2,160,3584]{2,1,0:T(8,128)(2,1)} %copy-done, bf16[2,160,3584]{2,1,0:T(8,128)(2,1)} %collective-permute-done.1.fy_ref, bf16[160,3584]{1,0:T(8,128)(2,1)} %copy-done.1, ...), custom_call_target="tpu_custom_call" | custom-call | flops 4587520 | bytes 16056320 | tf_op jit(solution)/shard_map/sum_rows/pallas_call | solution.py:499
Async XLA Ops:
  179.4 79.2 %collective-permute-start = (bf16[2,160,3584]{2,1,0:T(8,128)(2,1)}, bf16[2,160,3584]{2,1,0:T(8,128)(2,1)S(1)}, u32[]{:S(2)}, u32[]{:S(2)}) collective-permute-start(bf16[2,160,3584]{2,1,0:T(8,128)(2,1)} %get-tuple-element.23), channel_id=1, source_target_pairs={{0,4},{1,5},{2,6},{3,7},{4,0},{5,1},{6,2},{7,3}} | collective-permute-start | bytes 6881288 | tf_op jit(solution)/shard_map/ppermute | solution.py:518
  180.9 77.7 %collective-permute-start.1 = (bf16[2,160,3584]{2,1,0:T(8,128)(2,1)}, bf16[2,160,3584]{2,1,0:T(8,128)(2,1)}, u32[]{:S(2)}, u32[]{:S(2)}) collective-permute-start(bf16[2,160,3584]{2,1,0:T(8,128)(2,1)} %get-tuple-element.24), channel_id=1, source_target_pairs={{0,2},{1,3},{2,0},{3,1},{4,6},{5,7},{6,4},{7,5}} | collective-permute-start | bytes 6881288 | tf_op jit(solution)/shard_map/ppermute | solution.py:519
  258.6 1.4 copy-start
  264.0 42.4 %collective-permute-start.2 = (bf16[160,3584]{1,0:T(8,128)(2,1)}, bf16[160,3584]{1,0:T(8,128)(2,1)S(1)}, u32[]{:S(2)}, u32[]{:S(2)}) collective-permute-start(bf16[160,3584]{1,0:T(8,128)(2,1)} %get-tuple-element.29), channel_id=1, source_target_pairs={{0,4},{1,5},{2,6},{3,7},{4,0},{5,1},{6,2},{7,3}} | collective-permute-start | bytes 3440648 | tf_op jit(solution)/shard_map/ppermute | solution.py:524
  265.5 40.9 %collective-permute-start.3 = (bf16[160,3584]{1,0:T(8,128)(2,1)}, bf16[160,3584]{1,0:T(8,128)(2,1)S(1)}, u32[]{:S(2)}, u32[]{:S(2)}) collective-permute-start(bf16[160,3584]{1,0:T(8,128)(2,1)} %get-tuple-element.30), channel_id=1, source_target_pairs={{0,2},{1,3},{2,0},{3,1},{4,6},{5,7},{6,4},{7,5}} | collective-permute-start | bytes 3440648 | tf_op jit(solution)/shard_map/ppermute | solution.py:523
  306.4 1.0 copy-start.1
  306.4 1.5 copy-start.2

commit v6 on v5

--- a/solution.py
+++ b/solution.py
@@ -7,7 +7,7 @@
 
 MESH = pl.DeviceIdType.MESH
 ANY = pl.BlockSpec(memory_space=pl.ANY)
-VMEM_LIMIT = 60 * 2**20
+VMEM_LIMIT = 67043328
 C0 = 0.7978845608028654
 C1 = C0 * 0.044715
 
@@ -120,31 +120,32 @@
     ]
     where = [[block(*piece) for piece in part] for part in pieces]
 
-    def w_copies(tile, slot):
-        at = pl.ds(pl.multiple_of(tile * WTILE, WTILE), WTILE)
+    def w_rows(tile):
+        return pl.ds(pl.multiple_of(tile * WTILE, WTILE), WTILE)
+
+    def w_copies(tile):
+        at = w_rows(tile)
         return [
-            pltpu.make_async_copy(ref.at[at, :], wbuf.at[slot, i], w_sem.at[slot, i]) for i, ref in enumerate((wg_ref, wu_ref))
+            pltpu.make_async_copy(ref.at[at, :], wbuf.at[i, at, :], w_sem.at[tile, i]) for i, ref in enumerate((wg_ref, wu_ref))
         ]
 
-    def dx(k, last, parts, ins, outs, store, hooks, heights=None):
+    def dx(first_pass, parts, ins, outs, store, hooks, heights=None):
         def body(step, *refs):
             n = step.index[0]
-            slot = lax.rem(wtiles * k + n, 2)
-            for copy in w_copies(n, slot):
-                copy.wait()
-
-            def ahead():
-                for copy in w_copies(lax.rem(n + 1, wtiles), 1 - slot):
-                    copy.start()
-
-            if last:
-                pl.when(n < wtiles - 1)(ahead)
-            else:
-                ahead()
-            for at, hook in hooks.items():
-                pl.when(n == at)(hook)
+            at = w_rows(n)
+            if first_pass:
+                for copy in w_copies(n):
+                    copy.wait()
+
+                @pl.when(n + 3 < wtiles)
+                def _():
+                    for copy in w_copies(n + 3):
+                        copy.start()
+
+            for when, hook in hooks.items():
+                pl.when(n == when)(hook)
             sums = [
-                nt(dgc[p, pl.ds(first, count), :], wbuf[slot, 0]) + nt(duc[p, pl.ds(first, count), :], wbuf[slot, 1])
+                nt(dgc[p, pl.ds(first, count), :], wbuf[0, at, :]) + nt(duc[p, pl.ds(first, count), :], wbuf[1, at, :])
                 for p, first, count in parts
             ]
             store(sums, refs[: len(ins)], refs[len(ins) :])
@@ -160,11 +161,11 @@
             _explicit_indices=True,
         )(*ins, *outs)
 
-    def give(k, p, hooks={}):
+    def give(p, hooks={}):
         def store(sums, _, outs):
             outs[0][...] = sums[0].astype(jnp.bfloat16)
 
-        dx(k, False, [(p, 0, rows)], [], [give_ref.at[p]], store, hooks)
+        dx(False, [(p, 0, rows)], [], [give_ref.at[p]], store, hooks)
         pair(p).start()
 
     def with_acts(dyc, wdb, gub, hc):
@@ -175,9 +176,9 @@
                 src = dyf_ref.at[where[p][i], :]
             return pltpu.make_async_copy(src, dyc.at[pl.ds(i * half, half), :], dy_sem.at[i])
 
-        def wd_copy(j):
+        def wd_copy(j, slot):
             at = pl.ds(pl.multiple_of(j * TILE, TILE), TILE)
-            return pltpu.make_async_copy(wd_ref.at[at, :], wdb.at[at, :], wd_sem.at[j])
+            return pltpu.make_async_copy(wd_ref.at[at, :], wdb.at[slot], wd_sem.at[slot])
 
         def gu_copies(p):
             return [
@@ -204,10 +205,26 @@
                     copy.wait()
 
             def tile(j, carry):
+                count = tiles * p + j
+                slot = lax.rem(count, 2)
+                wd_copy(j, slot).wait()
+
+                def ahead():
+                    wd_copy(lax.rem(j + 1, tiles), 1 - slot).start()
+
+                if p < 3:
+                    ahead()
+                else:
+                    pl.when(j < tiles - 1)(ahead)
                 if p == 0:
-                    wd_copy(j).wait()
+
+                    @pl.when((j > 0) & (j < 4))
+                    def _():
+                        for copy in w_copies(j - 1):
+                            copy.start()
+
                 at = pl.ds(pl.multiple_of(j * TILE, TILE), TILE)
-                d_hidden = nt(dyc[...], wdb[at, :])
+                d_hidden = nt(dyc[...], wdb[slot])
                 h, dg, du = act_and_back(gub[0, :, at], gub[1, :, at], d_hidden)
                 dgc[p, :, at] = dg.astype(jnp.bfloat16)
                 duc[p, :, at] = du.astype(jnp.bfloat16)
@@ -238,18 +255,13 @@
         dys.send(0, 1, 4, 2, 3)
         dy_load(0, 2).start()
         dy_load(0, 3).start()
-        wd_copy(0).start()
+        wd_copy(0, 0).start()
         for copy in gu_copies(0):
             copy.start()
-        wd_copy(1).start()
         dys.arrived(0)
         dy_load(0, 0).start()
         dy_load(0, 1).start()
-        for j in range(2, tiles):
-            wd_copy(j).start()
         for copy in own_x(0):
-            copy.start()
-        for copy in w_copies(0, 0):
             copy.start()
         act(0)
         own_dy().start()
@@ -282,35 +294,35 @@
             outs[1][...] = sums[1]
 
         dx(
-            0, False, [(0, 0, rows), (0, rows, rows)], [], [give_ref.at[0], keep_s_ref], store_s,
+            True, [(0, 0, rows), (0, rows, rows)], [], [give_ref.at[0], keep_s_ref], store_s,
             {wtiles - 3: first_halves, wtiles - 1: load_first},
         )
         pair(0).start()
         act(1)
         dys.arrived(2, 3)
         dys.send(8, 9)
-        give(1, 1, {wtiles - 1: load(2, 8, 9)})
+        give(1, {wtiles - 1: load(2, 8, 9)})
         act(2)
 
         def far_halves():
             dys.arrived(5, 6)
             dys.send(11, 12)
 
-        give(2, 2, {wtiles - 4: far_halves, wtiles - 1: load(3, 11, 12)})
+        give(2, {wtiles - 4: far_halves, wtiles - 1: load(3, 11, 12)})
         act(3)
 
         def first_x_halves():
             xs.arrived(1, 4)
             xs.send(5, 6, 7, 10)
 
-        give(3, 3, {0: first_x_halves})
+        give(3, {0: first_x_halves})
         for copy in out_copies(3):
             copy.wait()
 
     pl.run_scoped(
         with_acts,
         pltpu.VMEM((2 * rows, d), jnp.bfloat16),
-        pltpu.VMEM((ff, d), jnp.bfloat16),
+        pltpu.VMEM((2, TILE, d), jnp.bfloat16),
         pltpu.VMEM((2, 2 * rows, ff), jnp.bfloat16),
         pltpu.VMEM((2 * rows, ff), jnp.bfloat16),
     )
@@ -330,7 +342,7 @@
         kept[...] = near1
 
     dx(
-        4, False, [(p, rows, rows) for p in (1, 2)], [got_ref.at[1], got_ref.at[2]],
+        False, [(p, rows, rows) for p in (1, 2)], [got_ref.at[1], got_ref.at[2]],
         [send_x_ref.at[0], send_y_ref.at[0], keep_n_ref], store_near, {0: second_halves}, [half, half, rows],
     )
     pair(3).wait_recv()
@@ -340,7 +352,7 @@
         outs[0][...] = total[:half].astype(jnp.bfloat16)
         outs[1][...] = total[half:].astype(jnp.bfloat16)
 
-    dx(5, True, [(3, rows, rows)], [got_ref.at[3]], [send_x_ref.at[1], send_y_ref.at[1]], store_far, {}, [half, half])
+    dx(False, [(3, rows, rows)], [got_ref.at[3]], [send_x_ref.at[1], send_y_ref.at[1]], store_far, {}, [half, half])
     xs.arrived(5, 6)
     xs.send(11, 12)
     xs.arrived(0, 7, 8, 9, 10, 11, 12)
@@ -369,9 +381,9 @@
         scratch_shapes=[
             pltpu.VMEM((4, 2 * rows, ff), bf16),
             pltpu.VMEM((4, 2 * rows, ff), bf16),
-            pltpu.VMEM((2, 2, WTILE, ff), bf16),
-            dma((2, 13)), dma((2, 13)), dma((4,)), dma((4,)), dma((2, 2)),
-            dma((4,)), dma((7,)), dma((2, 4)), dma((3, 4)), dma((3, 2)),
+            pltpu.VMEM((2, d, ff), bf16),
+            dma((2, 13)), dma((2, 13)), dma((4,)), dma((4,)), dma((d // WTILE, 2)),
+            dma((4,)), dma((2,)), dma((2, 4)), dma((3, 4)), dma((3, 2)),
         ],
         compiler_params=pltpu.CompilerParams(
             collective_id=0, has_side_effects=True, vmem_limit_bytes=VMEM_LIMIT

time: 314 us -> 298 us (0.949)
  Pallas kernels: 307 us -> 293 us
    pallas_call x1, Pallas kernels: 179 us -> 165 us  [front(): pl.pallas_call(front_kernel, out_shape=[jax.ShapeDtypeStruct(*s) for s in...]
  transfers between devices with their start and end apart: 4 -> 4, of which waited for: 0 -> 0; matrix products, arithmetic and copies ran while one was open for 0% -> 0% of each run, Pallas kernels for 37% -> 39%
where the time goes in v6:
time: 298 us
  Pallas kernels  293 us (98%)
  starting transfers between devices  4.07 us (1%)
    pallas_call x1, Pallas kernels, front(): pl.pallas_call(front_kernel, out_shape=[jax.ShapeDtypeStruct(*s) for s in...  165 us
    pallas_call x1, Pallas kernels, dw_two(): pl.pallas_call(kernel, out_shape=[jax.ShapeDtypeStruct((ff, d), jnp.bfloa...  77.1 us
    pallas_call x1, Pallas kernels, dw(): pl.pallas_call(dw_kernel, out_shape=jax.ShapeDtypeStruct((m, n), jnp.bflo...  40.4 us
    pallas_call x1, Pallas kernels, sum_rows(): pl.pallas_call(kernel, out_shape=jax.ShapeDtypeStruct((rows, d), jnp.bflo...  6.23 us
  transfers between devices with their start and end apart: 4, of which 0 were waited for; matrix products, arithmetic and copies ran while one was open for 0% of the time, Pallas kernels for 39%

profile of v6, /device:TPU:0, one launch (start us, length us, event | category | flops | bytes accessed | tf_op | source)
XLA Modules:
  0.0 297.9 jit_solution(15880878941530132922)
XLA Ops:
  0.6 165.3 %front.1 = (bf16[2560,3584]{1,0:T(8,128)(2,1)}, bf16[2560,3584]{1,0:T(8,128)(2,1)}, bf16[2560,1792]{1,0:T(8,128)(2,1)}, bf16[2560,1792]{1,0:T(8,128)(2,1)}, bf16...) custom-call(bf16[320,3584]{1,0:T(8,128)(2,1)} %dy_ref.1, ...), custom_call_target="tpu_custom_call" | custom-call | flops 98650030080 | bytes 314572800 | tf_op jit(solution)/shard_map/front/pallas_call | solution.py:376
  165.9 0.6 collective-permute-start
  166.5 1.5 collective-permute-start.1
  168.0 77.1 %dw_two.1 = (bf16[1792,3584]{1,0:T(8,128)(2,1)}, bf16[3584,1792]{1,0:T(8,128)(2,1)}) custom-call(bf16[2560,1792]{1,0:T(8,128)(2,1)} %get-tuple-element.31.h_ref, bf16[2560,3584]{1,0:T(8,128)(2,1)} %get-tuple-element.32.dy_ref, bf16[2560,3584]{1,0:T(8,128)(2,1)} %get-tuple-element.33.x_ref.a_ref, bf16[2560,1792]{1,0:T(8,128)(2,1)} %get-tuple-element.34.dg_hbm), custom_call_target="tpu_custom_call" | custom-call | flops 65766686720 | bytes 80740352 | tf_op jit(solution)/shard_map/dw_two/pallas_call | solution.py:453
  245.1 0.0 collective-permute-done.fx_ref
  245.1 0.0 collective-permute-done.1.fy_ref
  245.1 4.1 %sum_on.1 = (bf16[160,3584]{1,0:T(8,128)(2,1)}, bf16[160,3584]{1,0:T(8,128)(2,1)}) custom-call(f32[320,3584]{1,0:T(8,128)} %get-tuple-element.26.kept_ref, bf16[2,160,3584]{2,1,0:T(8,128)(2,1)} %collective-permute-done.fx_ref, bf16[2,160,3584]{2,1,0:T(8,128)(2,1)} %collective-permute-done.1.fy_ref), custom_call_target="tpu_custom_call" | custom-call | flops 1146880 | bytes 9175040 | tf_op jit(solution)/shard_map/sum_on/pallas_call | solution.py:486
  249.2 0.5 collective-permute-start.2
  249.8 1.5 collective-permute-start.3
  251.3 40.4 %dw.1 = bf16[3584,1792]{1,0:T(8,128)(2,1)} custom-call(bf16[2560,3584]{1,0:T(8,128)(2,1)} %get-tuple-element.33.x_ref.a_ref, bf16[2560,1792]{1,0:T(8,128)(2,1)} %get-tuple-element.36.b_ref), custom_call_target="tpu_custom_call" | custom-call | flops 32883343360 | bytes 40370176 | tf_op jit(solution)/shard_map/dw/pallas_call | solution.py:405
  291.6 0.0 collective-permute-done.2.lx_ref
  291.6 0.0 collective-permute-done.3.ly_ref
  291.6 6.2 %sum_rows.1 = bf16[320,3584]{1,0:T(8,128)(2,1)} custom-call(f32[320,3584]{1,0:T(8,128)} %get-tuple-element.21.kept_ref, bf16[4,320,3584]{2,1,0:T(8,128)(2,1)} %get-tuple-element.22.got_ref, bf16[2,160,3584]{2,1,0:T(8,128)(2,1)} %collective-permute-done.fx_ref, bf16[2,160,3584]{2,1,0:T(8,128)(2,1)} %collective-permute-done.1.fy_ref, ...), custom_call_target="tpu_custom_call" | custom-call | flops 4587520 | bytes 16056320 | tf_op jit(solution)/shard_map/sum_rows/pallas_call | solution.py:511
Async XLA Ops:
  165.9 79.2 %collective-permute-start = (bf16[2,160,3584]{2,1,0:T(8,128)(2,1)}, bf16[2,160,3584]{2,1,0:T(8,128)(2,1)}, u32[]{:S(2)}, u32[]{:S(2)}) collective-permute-start(bf16[2,160,3584]{2,1,0:T(8,128)(2,1)} %get-tuple-element.23), channel_id=1, source_target_pairs={{0,4},{1,5},{2,6},{3,7},{4,0},{5,1},{6,2},{7,3}} | collective-permute-start | bytes 6881288 | tf_op jit(solution)/shard_map/ppermute | solution.py:530
  166.5 78.6 %collective-permute-start.1 = (bf16[2,160,3584]{2,1,0:T(8,128)(2,1)}, bf16[2,160,3584]{2,1,0:T(8,128)(2,1)}, u32[]{:S(2)}, u32[]{:S(2)}) collective-permute-start(bf16[2,160,3584]{2,1,0:T(8,128)(2,1)} %get-tuple-element.24), channel_id=1, source_target_pairs={{0,2},{1,3},{2,0},{3,1},{4,6},{5,7},{6,4},{7,5}} | collective-permute-start | bytes 6881288 | tf_op jit(solution)/shard_map/ppermute | solution.py:531
  249.2 42.4 %collective-permute-start.2 = (bf16[160,3584]{1,0:T(8,128)(2,1)}, bf16[160,3584]{1,0:T(8,128)(2,1)}, u32[]{:S(2)}, u32[]{:S(2)}) collective-permute-start(bf16[160,3584]{1,0:T(8,128)(2,1)} %get-tuple-element.29), channel_id=1, source_target_pairs={{0,4},{1,5},{2,6},{3,7},{4,0},{5,1},{6,2},{7,3}} | collective-permute-start | bytes 3440648 | tf_op jit(solution)/shard_map/ppermute | solution.py:536
  249.8 41.9 %collective-permute-start.3 = (bf16[160,3584]{1,0:T(8,128)(2,1)}, bf16[160,3584]{1,0:T(8,128)(2,1)}, u32[]{:S(2)}, u32[]{:S(2)}) collective-permute-start(bf16[160,3584]{1,0:T(8,128)(2,1)} %get-tuple-element.30), channel_id=1, source_target_pairs={{0,2},{1,3},{2,0},{3,1},{4,6},{5,7},{6,4},{7,5}} | collective-permute-start | bytes 3440648 | tf_op jit(solution)/shard_map/ppermute | solution.py:535

commit v7 on v6

--- a/solution.py
+++ b/solution.py
@@ -36,7 +36,7 @@
 
 def front_kernel(
     dy_ref, x_ref, gate_ref, up_ref, wd_ref, wg_ref, wu_ref,
-    dyf_ref, xf_ref, dg_ref, du_ref, h_ref, give_ref, got_ref, keep_s_ref, keep_n_ref, send_x_ref, send_y_ref,
+    dyf_ref, xf_ref, dg_ref, du_ref, h_ref, give_ref, got_s_ref, got_ref, keep_s_ref, keep_n_ref, send_x_ref, send_y_ref,
     dgc, duc, wbuf, send_sem, recv_sem, pair_send, pair_recv, w_sem, dy_sem, wd_sem, gu_sem, out_sem, own_sem,
 ):
     rows, d = dy_ref.shape
@@ -55,28 +55,30 @@
         pl.semaphore_signal(barrier, inc=1, device_id={"tp": peer}, device_id_type=MESH)
     pl.semaphore_wait(barrier, 3)
 
-    def block(owner, part=None):
-        if part is None:
-            return pl.ds(pl.multiple_of(owner * rows, rows), rows)
-        return pl.ds(pl.multiple_of(owner * rows + part * half, half), half)
+    quarter = half // 2
+
+    def block(owner, start=0, count=rows):
+        return pl.ds(pl.multiple_of(owner * rows + start, count), count)
 
     routes = [
-        (me, None, other),
-        (me, 0, near_x), (me, 1, near_x), (me, 0, near_y), (me, 1, near_y),
-        (near_x, 0, near_y), (near_y, 1, near_x),
-        (near_x, 0, other), (near_x, 1, other), (near_y, 0, other), (near_y, 1, other),
-        (far, 0, other), (far, 1, other),
+        (me, 0, rows, other),
+        (me, 0, half, near_x), (me, half, half, near_x), (me, 0, half, near_y), (me, half, half, near_y),
+        (near_x, 0, quarter, near_y), (near_y, half, quarter, near_x),
+        (near_x, 0, half, other), (near_x, half, half, other), (near_y, 0, half, other), (near_y, half, half, other),
+        (far, 0, quarter, other), (far, half, quarter, other),
+        (near_x, quarter, quarter, near_y), (near_y, half + quarter, quarter, near_x),
+        (far, quarter, quarter, other), (far, half + quarter, quarter, other),
     ]
-    places = [block(owner, part) for owner, part, _ in routes]
+    places = [block(owner, start, count) for owner, start, count, _ in routes]
 
     class Gather:
         def __init__(self, a, own, full):
             self.a, self.own, self.full = a, own, full
 
         def copy(self, number):
-            _, part, peer = routes[number]
+            _, start, count, peer = routes[number]
             if number < 5:
-                src = self.own if part is None else self.own.at[pl.ds(part * half, half), :]
+                src = self.own.at[pl.ds(start, count), :]
             else:
                 src = self.full.at[places[number], :]
             return pltpu.make_async_remote_copy(
@@ -105,7 +107,7 @@
     def pair(p):
         return pltpu.make_async_remote_copy(
             src_ref=give_ref.at[p],
-            dst_ref=got_ref.at[p],
+            dst_ref=got_s_ref if p == 0 else got_ref.at[p - 1],
             send_sem=pair_send.at[p],
             recv_sem=pair_recv.at[p],
             device_id={"tp": other},
@@ -118,7 +120,7 @@
         [(near_x + across, 1), (near_y + across, 0), (near_x, 1), (near_y, 0)],
         [(far + across, 0), (far + across, 1), (far, 0), (far, 1)],
     ]
-    where = [[block(*piece) for piece in part] for part in pieces]
+    where = [[block(owner, part * half, half) for owner, part in some] for some in pieces]
 
     def w_rows(tile):
         return pl.ds(pl.multiple_of(tile * WTILE, WTILE), WTILE)
@@ -272,7 +274,7 @@
 
         def first_halves():
             dys.arrived(1, 4)
-            dys.send(5, 6, 7, 10)
+            dys.send(5, 6, 13, 14, 7, 10)
             xs.send(0, 1, 4, 2, 3)
 
         def load(p, *numbers):
@@ -305,15 +307,15 @@
         act(2)
 
         def far_halves():
-            dys.arrived(5, 6)
-            dys.send(11, 12)
-
-        give(2, {wtiles - 4: far_halves, wtiles - 1: load(3, 11, 12)})
+            dys.arrived(5, 6, 13, 14)
+            dys.send(11, 12, 15, 16)
+
+        give(2, {wtiles - 4: far_halves, wtiles - 1: load(3, 11, 12, 15, 16)})
         act(3)
 
         def first_x_halves():
             xs.arrived(1, 4)
-            xs.send(5, 6, 7, 10)
+            xs.send(5, 6, 13, 14, 7, 10)
 
         give(3, {0: first_x_halves})
         for copy in out_copies(3):
@@ -342,7 +344,7 @@
         kept[...] = near1
 
     dx(
-        False, [(p, rows, rows) for p in (1, 2)], [got_ref.at[1], got_ref.at[2]],
+        False, [(p, rows, rows) for p in (1, 2)], [got_ref.at[0], got_ref.at[1]],
         [send_x_ref.at[0], send_y_ref.at[0], keep_n_ref], store_near, {0: second_halves}, [half, half, rows],
     )
     pair(3).wait_recv()
@@ -352,10 +354,12 @@
         outs[0][...] = total[:half].astype(jnp.bfloat16)
         outs[1][...] = total[half:].astype(jnp.bfloat16)
 
-    dx(False, [(3, rows, rows)], [got_ref.at[3]], [send_x_ref.at[1], send_y_ref.at[1]], store_far, {}, [half, half])
+    dx(False, [(3, rows, rows)], [got_ref.at[2]], [send_x_ref.at[1], send_y_ref.at[1]], store_far, {}, [half, half])
     xs.arrived(5, 6)
     xs.send(11, 12)
-    xs.arrived(0, 7, 8, 9, 10, 11, 12)
+    xs.arrived(13, 14)
+    xs.send(15, 16)
+    xs.arrived(0, 7, 8, 9, 10, 11, 12, 15, 16)
     pair(0).wait_recv()
     for p in range(4):
         pair(p).wait_send()
@@ -369,7 +373,7 @@
     bf16, f32 = jnp.bfloat16, jnp.float32
     shapes = [
         ((tokens, d), bf16), ((tokens, d), bf16), ((tokens, ff), bf16), ((tokens, ff), bf16), ((tokens, ff), bf16),
-        ((4, rows, d), bf16), ((4, rows, d), bf16), ((rows, d), f32), ((rows, d), f32),
+        ((4, rows, d), bf16), ((rows, d), bf16), ((3, rows, d), bf16), ((rows, d), f32), ((rows, d), f32),
         ((2, rows // 2, d), bf16), ((2, rows // 2, d), bf16),
     ]
     dma = pltpu.SemaphoreType.DMA
@@ -382,7 +386,7 @@
             pltpu.VMEM((4, 2 * rows, ff), bf16),
             pltpu.VMEM((4, 2 * rows, ff), bf16),
             pltpu.VMEM((2, d, ff), bf16),
-            dma((2, 13)), dma((2, 13)), dma((4,)), dma((4,)), dma((d // WTILE, 2)),
+            dma((2, 17)), dma((2, 17)), dma((4,)), dma((4,)), dma((d // WTILE, 2)),
             dma((4,)), dma((2,)), dma((2, 4)), dma((3, 4)), dma((3, 2)),
         ],
         compiler_params=pltpu.CompilerParams(
@@ -411,7 +415,7 @@
             pl.BlockSpec((tokens, n), lambda i: (0, 0), pipeline_mode=pl.Buffered(1)),
         ],
         out_specs=pl.BlockSpec((tm, n), lambda i: (i, 0)),
-        compiler_params=pltpu.CompilerParams(dimension_semantics=("arbitrary",), vmem_limit_bytes=VMEM_LIMIT),
+        compiler_params=pltpu.CompilerParams(dimension_semantics=("arbitrary",), vmem_limit_bytes=52 * 2**20),
         cost_estimate=pl.CostEstimate(
             flops=2 * tokens * m * n, bytes_accessed=2 * (tokens * m + tokens * n + m * n), transcendentals=0
         ),
@@ -424,17 +428,24 @@
     d = dy.shape[1]
     steps = d // tile
 
-    def kernel(h_ref, dy_ref, x_ref, dg_hbm, down_ref, gate_ref, held, sem):
+    def kernel(dy_ref, x_ref, h_hbm, dg_hbm, down_ref, gate_ref, h_held, held, h_sem, sem):
         i = pl.program_id(0)
         load = pltpu.make_async_copy(dg_hbm, held, sem)
+        cuts = [pl.ds(c, 256) for c in range(0, ff, 256)]
+        pieces = [pltpu.make_async_copy(h_hbm.at[:, at], h_held.at[:, at], h_sem.at[j]) for j, at in enumerate(cuts)]
 
         @pl.when(i == 0)
         def _():
+            for piece in pieces:
+                piece.start()
             load.start()
-
-        @pl.when(i < steps)
+            for piece, at in zip(pieces, cuts):
+                piece.wait()
+                down_ref[at, :] = tn(h_held[:, at], dy_ref[...]).astype(down_ref.dtype)
+
+        @pl.when((i > 0) & (i < steps))
         def _():
-            down_ref[...] = tn(h_ref[...], dy_ref[...]).astype(down_ref.dtype)
+            down_ref[...] = tn(h_held[...], dy_ref[...]).astype(down_ref.dtype)
 
         @pl.when(i == steps - 1)
         def _():
@@ -455,22 +466,27 @@
         out_shape=[jax.ShapeDtypeStruct((ff, d), jnp.bfloat16), jax.ShapeDtypeStruct((d, ff), jnp.bfloat16)],
         grid=(2 * steps,),
         in_specs=[
-            pl.BlockSpec((tokens, ff), lambda i: (0, 0), pipeline_mode=pl.Buffered(1)),
             pl.BlockSpec((tokens, tile), lambda i: (0, first(i))),
             pl.BlockSpec((tokens, tile), lambda i: (0, second(i))),
+            ANY,
             ANY,
         ],
         out_specs=[
             pl.BlockSpec((ff, tile), lambda i: (0, first(i))),
             pl.BlockSpec((tile, ff), lambda i: (second(i), 0)),
         ],
-        scratch_shapes=[pltpu.VMEM((tokens, ff), jnp.bfloat16), pltpu.SemaphoreType.DMA(())],
-        compiler_params=pltpu.CompilerParams(dimension_semantics=("arbitrary",), vmem_limit_bytes=VMEM_LIMIT),
+        scratch_shapes=[
+            pltpu.VMEM((tokens, ff), jnp.bfloat16),
+            pltpu.VMEM((tokens, ff), jnp.bfloat16),
+            pltpu.SemaphoreType.DMA((ff // 256,)),
+            pltpu.SemaphoreType.DMA(()),
+        ],
+        compiler_params=pltpu.CompilerParams(dimension_semantics=("arbitrary",), vmem_limit_bytes=48 * 2**20),
         cost_estimate=pl.CostEstimate(
             flops=4 * tokens * d * ff, bytes_accessed=4 * (tokens * d + tokens * ff + d * ff), transcendentals=0
         ),
         name="dw_two",
-    )(h, dy, x, dg)
+    )(dy, x, h, dg)
 
 
 def sum_on(kept, from_x, from_y, tile=1792):
@@ -489,7 +505,7 @@
         grid=(d // tile,),
         in_specs=[pl.BlockSpec((rows, tile), lambda i: (0, i)), part, part],
         out_specs=[out, out],
-        compiler_params=pltpu.CompilerParams(dimension_semantics=("arbitrary",), vmem_limit_bytes=VMEM_LIMIT),
+        compiler_params=pltpu.CompilerParams(dimension_semantics=("arbitrary",), vmem_limit_bytes=20 * 2**20),
         cost_estimate=pl.CostEstimate(flops=rows * d, bytes_accessed=8 * rows * d, transcendentals=0),
         name="sum_on",
     )(kept, from_x, from_y)
@@ -502,7 +518,7 @@
     def kernel(kept_ref, got_ref, fx_ref, fy_ref, lx_ref, ly_ref, o_ref):
         f32 = jnp.float32
         for at, near, last in ((pl.ds(0, half), fx_ref, ly_ref), (pl.ds(half, half), fy_ref, lx_ref)):
-            total = kept_ref[at, :] + got_ref[0, at, :].astype(f32) + near[0].astype(f32) + last[...].astype(f32)
+            total = kept_ref[at, :] + got_ref[at, :].astype(f32) + near[0].astype(f32) + last[...].astype(f32)
             o_ref[at, :] = total.astype(o_ref.dtype)
 
     full = pl.BlockSpec((rows, tile), lambda i: (0, i))
@@ -512,9 +528,9 @@
         kernel,
         out_shape=jax.ShapeDtypeStruct((rows, d), jnp.bfloat16),
         grid=(d // tile,),
-        in_specs=[full, pl.BlockSpec((1, rows, tile), lambda i: (0, 0, i)), part, part, last, last],
+        in_specs=[full, full, part, part, last, last],
         out_specs=full,
-        compiler_params=pltpu.CompilerParams(dimension_semantics=("arbitrary",), vmem_limit_bytes=VMEM_LIMIT),
+        compiler_params=pltpu.CompilerParams(dimension_semantics=("arbitrary",), vmem_limit_bytes=20 * 2**20),
         cost_estimate=pl.CostEstimate(flops=4 * rows * d, bytes_accessed=14 * rows * d, transcendentals=0),
         name="sum_rows",
     )(kept, got, from_x, from_y, last_x, last_y)
@@ -526,7 +542,7 @@
     to_y = [(i, i ^ 2) for i in range(devices)]
 
     def step(x, dy, gate, up, wg, wu, wd):
-        dyf, xf, dg, du, h, _, got, keep_s, keep_n, send_x, send_y = front(dy, x, gate, up, wd, wg, wu)
+        dyf, xf, dg, du, h, _, got_s, _, keep_s, keep_n, send_x, send_y = front(dy, x, gate, up, wd, wg, wu)
         from_x = lax.ppermute(send_x, "tp", to_x)
         from_y = lax.ppermute(send_y, "tp", to_y)
         dw_down, dw_gate = dw_two(h, dyf, xf, dg)
@@ -535,7 +551,7 @@
         last_y = lax.ppermute(on_y, "tp", to_y)
         last_x = lax.ppermute(on_x, "tp", to_x)
         dw_up = dw(xf, du)
-        dx = sum_rows(keep_s, got, from_x, from_y, last_x, last_y)
+        dx = sum_rows(keep_s, got_s, from_x, from_y, last_x, last_y)
         return dx, dw_gate, dw_up, dw_down
 
     rows, cols, down = P(("dp", "tp"), None), P("dp", "tp"), P("tp", None)

time: 298 us -> 295 us (0.990)
  Pallas kernels: 293 us -> 290 us
  transfers between devices with their start and end apart: 4 -> 4, of which waited for: 0 -> 0; matrix products, arithmetic and copies ran while one was open for 0% -> 0% of each run, Pallas kernels for 39% -> 40%
where the time goes in v7:
time: 295 us
  Pallas kernels  290 us (98%)
  starting transfers between devices  4.09 us (1%)
    pallas_call x1, Pallas kernels, front(): pl.pallas_call(front_kernel, out_shape=[jax.ShapeDtypeStruct(*s) for s in...  165 us
    pallas_call x1, Pallas kernels, dw_two(): pl.pallas_call(kernel, out_shape=[jax.ShapeDtypeStruct((ff, d), jnp.bfloa...  77.3 us
    pallas_call x1, Pallas kernels, dw(): pl.pallas_call(dw_kernel, out_shape=jax.ShapeDtypeStruct((m, n), jnp.bflo...  40.4 us
  transfers between devices with their start and end apart: 4, of which 0 were waited for; matrix products, arithmetic and copies ran while one was open for 0% of the time, Pallas kernels for 40%

profile of v7, /device:TPU:0, one launch (start us, length us, event | category | flops | bytes accessed | tf_op | source)
XLA Modules:
  0.0 294.7 jit_solution(5930239678091640171)
XLA Ops:
  0.6 165.5 %front.1 = (bf16[2560,3584]{1,0:T(8,128)(2,1)}, bf16[2560,3584]{1,0:T(8,128)(2,1)}, bf16[2560,1792]{1,0:T(8,128)(2,1)}, bf16[2560,1792]{1,0:T(8,128)(2,1)}, bf16...) custom-call(bf16[320,3584]{1,0:T(8,128)(2,1)} %dy_ref.1, ...), custom_call_target="tpu_custom_call" | custom-call | flops 98650030080 | bytes 314572800 | tf_op jit(solution)/shard_map/front/pallas_call | solution.py:380
  166.1 0.6 collective-permute-start
  166.7 1.5 collective-permute-start.1
  168.2 0.0 copy-start
  168.2 77.3 %dw_two.1 = (bf16[1792,3584]{1,0:T(8,128)(2,1)}, bf16[3584,1792]{1,0:T(8,128)(2,1)}) custom-call(bf16[2560,3584]{1,0:T(8,128)(2,1)} %get-tuple-element.31.dy_ref, bf16[2560,3584]{1,0:T(8,128)(2,1)} %get-tuple-element.32.x_ref.a_ref, bf16[2560,1792]{1,0:T(8,128)(2,1)} %get-tuple-element.33.h_hbm, bf16[2560,1792]{1,0:T(8,128)(2,1)} %get-tuple-element.34.dg_hbm), custom_call_target="tpu_custom_call" | custom-call | flops 65766686720 | bytes 80740352 | tf_op jit(solution)/shard_map/dw_two/pallas_call | solution.py:464
  245.5 0.0 collective-permute-done.fx_ref
  245.5 0.0 collective-permute-done.1.fy_ref
  245.5 0.0 copy-done
  245.6 2.0 sum_on.1
  247.6 0.0 slice-start
  247.6 0.0 slice-start.1
  247.6 0.0 copy-start.1
  247.6 0.6 collective-permute-start.2
  248.1 1.5 collective-permute-start.3
  249.6 40.4 %dw.1 = bf16[3584,1792]{1,0:T(8,128)(2,1)} custom-call(bf16[2560,3584]{1,0:T(8,128)(2,1)} %get-tuple-element.32.x_ref.a_ref, bf16[2560,1792]{1,0:T(8,128)(2,1)} %get-tuple-element.36.b_ref), custom_call_target="tpu_custom_call" | custom-call | flops 32883343360 | bytes 40370176 | tf_op jit(solution)/shard_map/dw/pallas_call | solution.py:409
  290.0 0.0 collective-permute-done.2.lx_ref
  290.0 0.0 collective-permute-done.3.ly_ref
  290.0 0.0 slice-done
  290.0 0.0 slice-done.1
  290.0 0.0 copy-done.1
  290.0 4.6 %sum_rows.1 = bf16[320,3584]{1,0:T(8,128)(2,1)} custom-call(f32[320,3584]{1,0:T(8,128)S(1)} %bitcast.1, bf16[320,3584]{1,0:T(8,128)(2,1)S(1)} %copy-done.1, bf16[2,160,3584]{2,1,0:T(8,128)(2,1)S(1)} %collective-permute-done.fx_ref, bf16[2,160,3584]{2,1,0:T(8,128)(2,1)S(1)} %collective-permute-done.1.fy_ref, bf16[160,3584]{1,0:T(8,128)(2,1)} %collective-permute-done.2.lx_ref, ...), custom_call_target="tpu_custom_call" | custom-call | flops 4587520 | bytes 16056320 | tf_op jit(solution)/shard_map/sum_rows/pallas_call | solution.py:527
  (1 shorter events, 0.0 us)
Async XLA Ops:
  166.1 79.4 %collective-permute-start = (bf16[2,160,3584]{2,1,0:T(8,128)(2,1)}, bf16[2,160,3584]{2,1,0:T(8,128)(2,1)S(1)}, u32[]{:S(2)}, u32[]{:S(2)}) collective-permute-start(bf16[2,160,3584]{2,1,0:T(8,128)(2,1)} %get-tuple-element.23), channel_id=1, source_target_pairs={{0,4},{1,5},{2,6},{3,7},{4,0},{5,1},{6,2},{7,3}} | collective-permute-start | bytes 6881288 | tf_op jit(solution)/shard_map/ppermute | solution.py:546
  166.7 78.9 %collective-permute-start.1 = (bf16[2,160,3584]{2,1,0:T(8,128)(2,1)}, bf16[2,160,3584]{2,1,0:T(8,128)(2,1)S(1)}, u32[]{:S(2)}, u32[]{:S(2)}) collective-permute-start(bf16[2,160,3584]{2,1,0:T(8,128)(2,1)} %get-tuple-element.24), channel_id=1, source_target_pairs={{0,2},{1,3},{2,0},{3,1},{4,6},{5,7},{6,4},{7,5}} | collective-permute-start | bytes 6881288 | tf_op jit(solution)/shard_map/ppermute | solution.py:547
  168.2 77.4 %copy-start = (f32[320,3584]{1,0:T(8,128)S(1)}, f32[320,3584]{1,0:T(8,128)}, u32[]{:S(2)}) copy-start(f32[320,3584]{1,0:T(8,128)} %get-tuple-element.26.kept_ref) | copy-start | bytes 13762564
  247.6 42.4 %slice-start = ((s8[4587520]{0:T(1024)(128)(4,1)}), s8[4194304]{0:T(1024)(128)(4,1)S(1)}, s32[]{:S(2)}) async-start(s8[4587520]{0:T(1024)(128)(4,1)} %bitcast), calls=%async_computation | async-start | bytes 8388608
  247.6 42.4 %slice-start.1 = ((s8[4587520]{0:T(1024)(128)(4,1)}), s8[393216]{0:T(1024)(128)(4,1)S(1)}, s32[]{:S(2)}) async-start(s8[4587520]{0:T(1024)(128)(4,1)} %bitcast), calls=%async_computation.1 | async-start | bytes 786432
  247.6 42.4 %copy-start.1 = (bf16[320,3584]{1,0:T(8,128)(2,1)S(1)}, bf16[320,3584]{1,0:T(8,128)(2,1)}, u32[]{:S(2)}) copy-start(bf16[320,3584]{1,0:T(8,128)(2,1)} %get-tuple-element.22.got_ref) | copy-start | bytes 6881284
  247.6 42.4 %collective-permute-start.2 = (bf16[160,3584]{1,0:T(8,128)(2,1)}, bf16[160,3584]{1,0:T(8,128)(2,1)}, u32[]{:S(2)}, u32[]{:S(2)}) collective-permute-start(bf16[160,3584]{1,0:T(8,128)(2,1)} %get-tuple-element.29), channel_id=1, source_target_pairs={{0,4},{1,5},{2,6},{3,7},{4,0},{5,1},{6,2},{7,3}} | collective-permute-start | bytes 3440648 | tf_op jit(solution)/shard_map/ppermute | solution.py:552
  248.1 41.9 %collective-permute-start.3 = (bf16[160,3584]{1,0:T(8,128)(2,1)}, bf16[160,3584]{1,0:T(8,128)(2,1)}, u32[]{:S(2)}, u32[]{:S(2)}) collective-permute-start(bf16[160,3584]{1,0:T(8,128)(2,1)} %get-tuple-element.30), channel_id=1, source_target_pairs={{0,2},{1,3},{2,0},{3,1},{4,6},{5,7},{6,4},{7,5}} | collective-permute-start | bytes 3440648 | tf_op jit(solution)/shard_map/ppermute | solution.py:551

commit v8 on v7

--- a/solution.py
+++ b/solution.py
@@ -55,30 +55,28 @@
         pl.semaphore_signal(barrier, inc=1, device_id={"tp": peer}, device_id_type=MESH)
     pl.semaphore_wait(barrier, 3)
 
-    quarter = half // 2
-
-    def block(owner, start=0, count=rows):
-        return pl.ds(pl.multiple_of(owner * rows + start, count), count)
+    def block(owner, part=None):
+        if part is None:
+            return pl.ds(pl.multiple_of(owner * rows, rows), rows)
+        return pl.ds(pl.multiple_of(owner * rows + part * half, half), half)
 
     routes = [
-        (me, 0, rows, other),
-        (me, 0, half, near_x), (me, half, half, near_x), (me, 0, half, near_y), (me, half, half, near_y),
-        (near_x, 0, quarter, near_y), (near_y, half, quarter, near_x),
-        (near_x, 0, half, other), (near_x, half, half, other), (near_y, 0, half, other), (near_y, half, half, other),
-        (far, 0, quarter, other), (far, half, quarter, other),
-        (near_x, quarter, quarter, near_y), (near_y, half + quarter, quarter, near_x),
-        (far, quarter, quarter, other), (far, half + quarter, quarter, other),
+        (me, None, other),
+        (me, 0, near_x), (me, 1, near_x), (me, 0, near_y), (me, 1, near_y),
+        (near_x, 0, near_y), (near_y, 1, near_x),
+        (near_x, 0, other), (near_x, 1, other), (near_y, 0, other), (near_y, 1, other),
+        (far, 0, other), (far, 1, other),
     ]
-    places = [block(owner, start, count) for owner, start, count, _ in routes]
+    places = [block(owner, part) for owner, part, _ in routes]
 
     class Gather:
         def __init__(self, a, own, full):
             self.a, self.own, self.full = a, own, full
 
         def copy(self, number):
-            _, start, count, peer = routes[number]
+            _, part, peer = routes[number]
             if number < 5:
-                src = self.own.at[pl.ds(start, count), :]
+                src = self.own if part is None else self.own.at[pl.ds(part * half, half), :]
             else:
                 src = self.full.at[places[number], :]
             return pltpu.make_async_remote_copy(
@@ -120,7 +118,7 @@
         [(near_x + across, 1), (near_y + across, 0), (near_x, 1), (near_y, 0)],
         [(far + across, 0), (far + across, 1), (far, 0), (far, 1)],
     ]
-    where = [[block(owner, part * half, half) for owner, part in some] for some in pieces]
+    where = [[block(*piece) for piece in part] for part in pieces]
 
     def w_rows(tile):
         return pl.ds(pl.multiple_of(tile * WTILE, WTILE), WTILE)
@@ -274,7 +272,7 @@
 
         def first_halves():
             dys.arrived(1, 4)
-            dys.send(5, 6, 13, 14, 7, 10)
+            dys.send(5, 6, 7, 10)
             xs.send(0, 1, 4, 2, 3)
 
         def load(p, *numbers):
@@ -307,15 +305,15 @@
         act(2)
 
         def far_halves():
-            dys.arrived(5, 6, 13, 14)
-            dys.send(11, 12, 15, 16)
-
-        give(2, {wtiles - 4: far_halves, wtiles - 1: load(3, 11, 12, 15, 16)})
+            dys.arrived(5, 6)
+            dys.send(11, 12)
+
+        give(2, {wtiles - 4: far_halves, wtiles - 1: load(3, 11, 12)})
         act(3)
 
         def first_x_halves():
             xs.arrived(1, 4)
-            xs.send(5, 6, 13, 14, 7, 10)
+            xs.send(5, 6, 7, 10)
 
         give(3, {0: first_x_halves})
         for copy in out_copies(3):
@@ -357,9 +355,7 @@
     dx(False, [(3, rows, rows)], [got_ref.at[2]], [send_x_ref.at[1], send_y_ref.at[1]], store_far, {}, [half, half])
     xs.arrived(5, 6)
     xs.send(11, 12)
-    xs.arrived(13, 14)
-    xs.send(15, 16)
-    xs.arrived(0, 7, 8, 9, 10, 11, 12, 15, 16)
+    xs.arrived(0, 7, 8, 9, 10, 11, 12)
     pair(0).wait_recv()
     for p in range(4):
         pair(p).wait_send()
@@ -386,7 +382,7 @@
             pltpu.VMEM((4, 2 * rows, ff), bf16),
             pltpu.VMEM((4, 2 * rows, ff), bf16),
             pltpu.VMEM((2, d, ff), bf16),
-            dma((2, 17)), dma((2, 17)), dma((4,)), dma((4,)), dma((d // WTILE, 2)),
+            dma((2, 13)), dma((2, 13)), dma((4,)), dma((4,)), dma((d // WTILE, 2)),
             dma((4,)), dma((2,)), dma((2, 4)), dma((3, 4)), dma((3, 2)),
         ],
         compiler_params=pltpu.CompilerParams(
@@ -511,7 +507,7 @@
     )(kept, from_x, from_y)
 
 
-def sum_rows(kept, got, from_x, from_y, last_x, last_y, tile=896):
+def sum_rows(kept, got, from_x, from_y, last_x, last_y):
     rows, d = kept.shape
     half = rows // 2
 
@@ -521,16 +517,12 @@
             total = kept_ref[at, :] + got_ref[at, :].astype(f32) + near[0].astype(f32) + last[...].astype(f32)
             o_ref[at, :] = total.astype(o_ref.dtype)
 
-    full = pl.BlockSpec((rows, tile), lambda i: (0, i))
-    part = pl.BlockSpec((1, half, tile), lambda i: (0, 0, i))
-    last = pl.BlockSpec((half, tile), lambda i: (0, i))
     return pl.pallas_call(
         kernel,
         out_shape=jax.ShapeDtypeStruct((rows, d), jnp.bfloat16),
-        grid=(d // tile,),
-        in_specs=[full, full, part, part, last, last],
-        out_specs=full,
-        compiler_params=pltpu.CompilerParams(dimension_semantics=("arbitrary",), vmem_limit_bytes=20 * 2**20),
+        in_specs=[pl.BlockSpec(memory_space=pltpu.VMEM)] * 6,
+        out_specs=pl.BlockSpec(memory_space=pltpu.VMEM),
+        compiler_params=pltpu.CompilerParams(vmem_limit_bytes=20 * 2**20),
         cost_estimate=pl.CostEstimate(flops=4 * rows * d, bytes_accessed=14 * rows * d, transcendentals=0),
         name="sum_rows",
     )(kept, got, from_x, from_y, last_x, last_y)

time: 295 us -> 294 us (level)
  no operation moved by 1% of the time
where the time goes in v8:
time: 294 us
  Pallas kernels  289 us (98%)
  starting transfers between devices  4.09 us (1%)
    pallas_call x1, Pallas kernels, front(): pl.pallas_call(front_kernel, out_shape=[jax.ShapeDtypeStruct(*s) for s in...  165 us
    pallas_call x1, Pallas kernels, dw_two(): pl.pallas_call(kernel, out_shape=[jax.ShapeDtypeStruct((ff, d), jnp.bfloa...  77.3 us
    pallas_call x1, Pallas kernels, dw(): pl.pallas_call(dw_kernel, out_shape=jax.ShapeDtypeStruct((m, n), jnp.bflo...  40.4 us
  transfers between devices with their start and end apart: 4, of which 0 were waited for; matrix products, arithmetic and copies ran while one was open for 0% of the time, Pallas kernels for 40%

profile of v8, /device:TPU:0, one launch (start us, length us, event | category | flops | bytes accessed | tf_op | source)
XLA Modules:
  0.0 293.8 jit_solution(4699578170132661436)
XLA Ops:
  0.6 165.3 %front.1 = (bf16[2560,3584]{1,0:T(8,128)(2,1)}, bf16[2560,3584]{1,0:T(8,128)(2,1)}, bf16[2560,1792]{1,0:T(8,128)(2,1)}, bf16[2560,1792]{1,0:T(8,128)(2,1)}, bf16...) custom-call(bf16[320,3584]{1,0:T(8,128)(2,1)} %dy_ref.1, ...), custom_call_target="tpu_custom_call" | custom-call | flops 98650030080 | bytes 314572800 | tf_op jit(solution)/shard_map/front/pallas_call | solution.py:376
  166.0 0.6 collective-permute-start
  166.5 1.5 collective-permute-start.1
  168.0 0.0 copy-start
  168.0 77.3 %dw_two.1 = (bf16[1792,3584]{1,0:T(8,128)(2,1)}, bf16[3584,1792]{1,0:T(8,128)(2,1)}) custom-call(bf16[2560,3584]{1,0:T(8,128)(2,1)} %get-tuple-element.31.dy_ref, bf16[2560,3584]{1,0:T(8,128)(2,1)} %get-tuple-element.32.x_ref.a_ref, bf16[2560,1792]{1,0:T(8,128)(2,1)} %get-tuple-element.33.h_hbm, bf16[2560,1792]{1,0:T(8,128)(2,1)} %get-tuple-element.34.dg_hbm), custom_call_target="tpu_custom_call" | custom-call | flops 65766686720 | bytes 80740352 | tf_op jit(solution)/shard_map/dw_two/pallas_call | solution.py:460
  245.4 0.0 collective-permute-done.fx_ref
  245.4 0.0 collective-permute-done.1.fy_ref
  245.4 0.0 copy-done
  245.4 2.0 sum_on.1
  247.4 0.0 slice-start
  247.4 0.0 slice-start.1
  247.4 0.0 copy-start.1
  247.4 0.6 collective-permute-start.2
  248.0 1.5 collective-permute-start.3
  249.5 40.4 %dw.1 = bf16[3584,1792]{1,0:T(8,128)(2,1)} custom-call(bf16[2560,3584]{1,0:T(8,128)(2,1)} %get-tuple-element.32.x_ref.a_ref, bf16[2560,1792]{1,0:T(8,128)(2,1)} %get-tuple-element.36.b_ref), custom_call_target="tpu_custom_call" | custom-call | flops 32883343360 | bytes 40370176 | tf_op jit(solution)/shard_map/dw/pallas_call | solution.py:405
  289.8 0.0 collective-permute-done.2.lx_ref
  289.8 0.0 collective-permute-done.3.ly_ref
  289.8 0.0 slice-done
  289.8 0.0 slice-done.1
  289.9 0.0 copy-done.1
  289.9 4.0 %sum_rows.1 = bf16[320,3584]{1,0:T(8,128)(2,1)} custom-call(f32[320,3584]{1,0:T(8,128)S(1)} %bitcast.1, bf16[320,3584]{1,0:T(8,128)(2,1)S(1)} %copy-done.1, bf16[2,160,3584]{2,1,0:T(8,128)(2,1)S(1)} %collective-permute-done.fx_ref, bf16[2,160,3584]{2,1,0:T(8,128)(2,1)S(1)} %collective-permute-done.1.fy_ref, bf16[160,3584]{1,0:T(8,128)(2,1)} %collective-permute-done.2.lx_ref, ...), custom_call_target="tpu_custom_call" | custom-call | flops 4587520 | bytes 16056320 | tf_op jit(solution)/shard_map/sum_rows/pallas_call | solution.py:520
  (1 shorter events, 0.0 us)
Async XLA Ops:
  166.0 79.4 %collective-permute-start = (bf16[2,160,3584]{2,1,0:T(8,128)(2,1)}, bf16[2,160,3584]{2,1,0:T(8,128)(2,1)S(1)}, u32[]{:S(2)}, u32[]{:S(2)}) collective-permute-start(bf16[2,160,3584]{2,1,0:T(8,128)(2,1)} %get-tuple-element.23), channel_id=1, source_target_pairs={{0,4},{1,5},{2,6},{3,7},{4,0},{5,1},{6,2},{7,3}} | collective-permute-start | bytes 6881288 | tf_op jit(solution)/shard_map/ppermute | solution.py:538
  166.5 78.9 %collective-permute-start.1 = (bf16[2,160,3584]{2,1,0:T(8,128)(2,1)}, bf16[2,160,3584]{2,1,0:T(8,128)(2,1)S(1)}, u32[]{:S(2)}, u32[]{:S(2)}) collective-permute-start(bf16[2,160,3584]{2,1,0:T(8,128)(2,1)} %get-tuple-element.24), channel_id=1, source_target_pairs={{0,2},{1,3},{2,0},{3,1},{4,6},{5,7},{6,4},{7,5}} | collective-permute-start | bytes 6881288 | tf_op jit(solution)/shard_map/ppermute | solution.py:539
  168.0 77.4 %copy-start = (f32[320,3584]{1,0:T(8,128)S(1)}, f32[320,3584]{1,0:T(8,128)}, u32[]{:S(2)}) copy-start(f32[320,3584]{1,0:T(8,128)} %get-tuple-element.26.kept_ref) | copy-start | bytes 13762564
  247.4 42.4 %slice-start = ((s8[4587520]{0:T(1024)(128)(4,1)}), s8[4194304]{0:T(1024)(128)(4,1)S(1)}, s32[]{:S(2)}) async-start(s8[4587520]{0:T(1024)(128)(4,1)} %bitcast), calls=%async_computation | async-start | bytes 8388608
  247.4 42.4 %slice-start.1 = ((s8[4587520]{0:T(1024)(128)(4,1)}), s8[393216]{0:T(1024)(128)(4,1)S(1)}, s32[]{:S(2)}) async-start(s8[4587520]{0:T(1024)(128)(4,1)} %bitcast), calls=%async_computation.1 | async-start | bytes 786432
  247.4 42.4 %copy-start.1 = (bf16[320,3584]{1,0:T(8,128)(2,1)S(1)}, bf16[320,3584]{1,0:T(8,128)(2,1)}, u32[]{:S(2)}) copy-start(bf16[320,3584]{1,0:T(8,128)(2,1)} %get-tuple-element.22.got_ref) | copy-start | bytes 6881284
  247.4 42.4 %collective-permute-start.2 = (bf16[160,3584]{1,0:T(8,128)(2,1)}, bf16[160,3584]{1,0:T(8,128)(2,1)}, u32[]{:S(2)}, u32[]{:S(2)}) collective-permute-start(bf16[160,3584]{1,0:T(8,128)(2,1)} %get-tuple-element.29), channel_id=1, source_target_pairs={{0,4},{1,5},{2,6},{3,7},{4,0},{5,1},{6,2},{7,3}} | collective-permute-start | bytes 3440648 | tf_op jit(solution)/shard_map/ppermute | solution.py:544
  248.0 41.9 %collective-permute-start.3 = (bf16[160,3584]{1,0:T(8,128)(2,1)}, bf16[160,3584]{1,0:T(8,128)(2,1)}, u32[]{:S(2)}, u32[]{:S(2)}) collective-permute-start(bf16[160,3584]{1,0:T(8,128)(2,1)} %get-tuple-element.30), channel_id=1, source_target_pairs={{0,2},{1,3},{2,0},{3,1},{4,6},{5,7},{6,4},{7,5}} | collective-permute-start | bytes 3440648 | tf_op jit(solution)/shard_map/ppermute | solution.py:543
